TPU v7x, 128 devices: a whole 4x4x4 slice. The times are simulated.
128 devices in a mesh: seq: 16 (over z, x_lo, core), tp: 8 (over y, x_hi).
Axes of the slice: x: 4 (x_hi: 2, x_lo: 2; x = x_hi * 2 + x_lo), y: 4, z: 4, core: 2. Of those that a mesh axis runs over, the one named last changes fastest.
Arguments:
- hidden_in: bfloat16 [8192, 4608], P('seq'), may hold values from -6 to 6
- pre_gain: float32 [4608], replicated, may hold values from 0.5 to 1.5
- w_query: bfloat16 [4608, 4096], P(None, 'tp'), may hold values from -0.09375 to 0.09375
- key_cache: bfloat16 [16384, 2048], P('seq', 'tp'), may hold values from -12 to 12
- value_cache: bfloat16 [16384, 2048], P('seq', 'tp'), may hold values from -6 to 6
- w_out: bfloat16 [4096, 4608], P('tp'), may hold values from -0.75 to 0.75
- post_gain: float32 [4608], replicated, may hold values from 0.5 to 1.5
- starts: int32 [16], replicated, may hold values from 0 to 15872, as said below
- counts: int32 [16], replicated, may hold values from 512 to 1024, as said below
Outputs:
- layer_out: bfloat16 [8192, 4608], P(('seq', 'tp'))
Inputs may be any that keep to these rules, and one draw needn't show every extreme that they name: The queries of shard s sit at positions starts[s] to starts[s] + 511, all inside the filled rows of shard s, that is from s * 1024 to s * 1024 + counts[s] - 1. `counts`: at least one shard is full.
All inputs are finite; a program needn't handle non-finite values.
Results may differ from a plain program's by a relative error of at most 0.012.
Values may be sent and summed in bfloat16 or wider, within the bound.
A program may use at most 128 MiB of HBM per device.

v0:
```python
import jax
import jax.numpy as jnp
from jax import lax
from jax.sharding import Mesh
from jax.sharding import PartitionSpec as P

D = 4608
H = 32
HD = 128
WINDOW = 4096
HALO = 4
TP = ("tp_0", "tp_1")
SEQ_TP = ("seq", "tp_0", "tp_1")


def passed_along(block, axis, distance):
    devices = range(lax.axis_size(axis))
    route = [(i - distance, i) for i in devices if i - distance in devices]
    return lax.ppermute(block, axis, route)


def summed_rows(terms, axes):
    total = terms.astype(jnp.bfloat16)
    for axis in axes:
        total = lax.psum_scatter(total, axis, scatter_dimension=0, tiled=True)
    return total.astype(jnp.float32)


def shards(hidden_in, pre_gain, w_query, key_cache, value_cache, w_out, post_gain, starts, counts):
    seq_count = lax.axis_size("seq")
    own_shard = lax.axis_index("seq")
    query_rows = hidden_in.shape[0]
    cache_rows = key_cache.shape[0]
    kv_local = key_cache.shape[1] // HD
    heads_local = w_query.shape[1] // HD
    per_group = heads_local // kv_local
    inputs = hidden_in.astype(jnp.float32)
    normed = (
        inputs * lax.rsqrt(jnp.mean(inputs * inputs, axis=-1, keepdims=True) + 0.1) * pre_gain
    ).astype(jnp.bfloat16)
    queries = (
        jnp.dot(normed, w_query, preferred_element_type=jnp.float32) * (D // H) ** (-0.5)
    ).astype(jnp.bfloat16)
    queries = queries.reshape(query_rows, kv_local, per_group, HD)
    query_pos = lax.dynamic_index_in_dim(starts, own_shard, 0, keepdims=False) + jnp.arange(
        query_rows, dtype=jnp.int32
    )
    row_ids = jnp.arange(cache_rows, dtype=jnp.int32)

    def attend(running, stacked, source):
        key_pos = source * cache_rows + row_ids
        source_clip = jnp.clip(source, 0, seq_count - 1)
        filled_rows = lax.dynamic_index_in_dim(counts, source_clip, 0, keepdims=False)
        filled = (source >= 0) & (row_ids < filled_rows)
        allowed = (
            filled[None, :]
            & (key_pos[None, :] <= query_pos[:, None])
            & (key_pos[None, :] > query_pos[:, None] - WINDOW)
        )
        key_block = stacked[0].reshape(cache_rows, kv_local, HD)
        value_block = stacked[1].reshape(cache_rows, kv_local, HD)
        scores = jnp.einsum(
            "qkgd,ckd->kgqc", queries, key_block, preferred_element_type=jnp.float32
        )
        scores = 50.0 * jnp.tanh(scores / 50.0)
        weight = jnp.where(allowed[None, None], jnp.exp(scores), jnp.float32(0.0))
        denominator, context = running
        denominator = denominator + jnp.sum(weight, axis=-1)
        context = context + jnp.einsum(
            "kgqc,ckd->qkgd",
            weight.astype(jnp.bfloat16),
            value_block,
            preferred_element_type=jnp.float32,
        )
        return (denominator, context)

    running = (
        jnp.zeros((kv_local, per_group, query_rows), jnp.float32),
        jnp.zeros((query_rows, kv_local, per_group, HD), jnp.float32),
    )
    own_cache = jnp.stack([key_cache, value_cache])
    running = attend(running, own_cache, own_shard)
    moving = own_cache
    for distance in range(1, HALO + 1):
        moving = passed_along(moving, "seq", 1)
        running = attend(running, moving, own_shard - distance)
    denominator, context = running
    attended = (
        (context / jnp.transpose(denominator, (2, 0, 1))[..., None])
        .reshape(query_rows, heads_local * HD)
        .astype(jnp.bfloat16)
    )
    block_rows = query_rows // lax.axis_size(TP)
    tp_place = lax.axis_index(TP)
    projected = summed_rows(jnp.dot(attended, w_out, preferred_element_type=jnp.float32), TP)
    residual = lax.dynamic_slice_in_dim(inputs, tp_place * block_rows, block_rows, 0)
    mixed_rows = (
        residual
        + projected
        * lax.rsqrt(jnp.mean(projected * projected, axis=-1, keepdims=True) + 0.1)
        * post_gain
    )
    return mixed_rows.astype(jnp.bfloat16)


def solution(mesh):
    finer = Mesh(mesh.devices.reshape(mesh.shape["seq"], 4, 2), ("seq", "tp_0", "tp_1"))
    in_specs = (
        P("seq", None),
        P(),
        P(None, TP),
        P("seq", TP),
        P("seq", TP),
        P(TP, None),
        P(),
        P(),
        P(),
    )
    out_specs = P(SEQ_TP, None)
    return jax.shard_map(
        shards, mesh=finer, in_specs=in_specs, out_specs=out_specs, check_vma=False
    )
```

profile of v0, /device:TPU:32, one launch (start us, length us, event | category | flops | bytes accessed | tf_op | source)
XLA Modules:
  0.0 198.1 jit_solution(5999997551407299927)
XLA Ops:
  6.5 0.0 copy-start.3
  6.5 0.0 copy-start.4
  6.5 0.0 reduce-scatter.3.cloned.1.call-start
  6.5 1.3 copy.71
  7.8 1.2 copy.32
  9.1 1.1 pad_maximum_fusion
  10.2 1.9 collective-permute-start
  12.1 2.0 reshape_squeeze_stack.6
  14.1 1.3 dynamic_slice.24
  15.4 0.6 iota_add_fusion.5
  16.1 3.3 %multiply_reduce_fusion = f32[512]{0:T(512)S(1)} fusion(bf16[512,4608]{1,0:T(8,128)(2,1)} %param.9), kind=kLoop, calls=%fused_computation.1 | loop fusion | flops 7077376 | bytes 4720640 | tf_op jit(solution)/shard_map/reduce_sum | solution.py:39
  19.4 0.0 copy-done.3
  19.4 0.7 fusion.85
  20.1 0.6 fusion.65
  20.8 1.4 fusion.61
  22.1 1.2 fusion.63
  23.3 3.0 %compare_and_fusion = (pred[512,1024]{1,0:T(8,128)(4,1)S(1)}, pred[512,1024]{1,0:T(8,128)(4,1)S(1)}, pred[512,1024]{1,0:T(8,128)(4,1)S(1)}, pred[512,1024]{1,0:T(8,128)(4,1)S(1)}, pred[512,1024]{1,0:T(8,128)(4,1)S(1)}) fusion(s32[1024]{0:T(1024)S(1)} %get-tuple-element.35, pred[1024]{0:T(1024)(128)(4,1)S(1)} %fusion.65, s32[512]{0:T(512)S(1)} %get-tuple-element.34, ...), kind=kLoop, calls=%fused_computation.32 | loop fusion | flops 10485760 | bytes 2651136 | tf_op jit(solution)/shard_map/and | solution.py:56
  26.3 1.5 copy.34
  27.8 0.9 copy.38
  28.6 0.9 copy.42
  29.5 0.9 copy.46
  30.4 0.0 copy-done.4
  30.4 0.0 copy-start
  30.4 6.6 %fusion.52 = bf16[512,512]{0,1:T(8,128)(2,1)S(1)} fusion(bf16[4608,512]{1,0:T(8,128)(2,1)} %param.11, f32[4608]{0:T(1024)S(1)} %copy-done.4, f32[512]{0:T(512)S(1)} %add_rsqrt_fusion, bf16[512,4608]{1,0:T(8,128)(2,1)} %param.9), kind=kOutput, calls=%fused_computation.49 | convolution fusion | flops 2425880576 | bytes 9981952 | tf_op jit(solution)/shard_map/dot_general | solution.py:42
  37.0 0.0 copy-done
  37.0 3.7 %bitcast_reduce_fusion = (f32[2,2,512]{2,1,0:T(2,128)S(1)}, f32[2,512,2,1024]{3,1,2,0:T(8,128)S(1)}) fusion(pred[512,1024]{1,0:T(8,128)(4,1)S(1)} %get-tuple-element.17, bf16[512,2,2,128]{0,3,2,1:T(8,128)(2,1)S(1)} %bitcast.162, bf16[1024,2,128,1]{2,1,0,3:T(2,128)(2,1)S(1)} %bitcast.153), kind=kOutput, calls=%fused_computation.6 | convolution fusion | flops 545257472 | bytes 9969664 | tf_op jit(solution)/shard_map/qkgd,ckd->kgqc/dot_general | solution.py:62
  40.7 0.0 copy-start.1
  40.7 2.7 %fusion.26 = f32[512,2,2,128]{0,3,2,1:T(8,128)S(1)} fusion(bf16[1024,2,128,1]{0,2,3,1:T(8,128)(2,1)S(1)} %bitcast.150, f32[2,512,2,1024]{3,1,2,0:T(8,128)S(1)} %get-tuple-element.30, pred[512,1024]{1,0:T(8,128)(4,1)S(1)} %get-tuple-element.17), kind=kOutput, calls=%fused_computation.39 | convolution fusion | flops 545259520 | bytes 10485760 | tf_op jit(solution)/shard_map/kgqc,ckd->qkgd/dot_general | solution.py:69
  43.4 0.0 collective-permute-done
  43.4 1.3 fusion.84
  44.7 3.7 %collective-permute-start.1 = (bf16[2,1024,256]{1,2,0:T(8,128)(2,1)}, bf16[2,1024,256]{1,2,0:T(8,128)(2,1)S(1)}, u32[]{:S(2)}, u32[]{:S(2)}) collective-permute-start(bf16[2,1024,256]{1,2,0:T(8,128)(2,1)} %collective-permute-done), channel_id=1, source_target_pairs={{0,8},{8,16},{16,24},{24,32},{32,40},{40,48},{48,56},{56,64},{64,7... | collective-permute-start | bytes 3145736 | tf_op jit(solution)/shard_map/ppermute | solution.py:19
  48.4 0.0 copy-done.1
  48.4 2.8 %fusion = (f32[2,2,512]{2,1,0:T(2,128)S(1)}, f32[2,1024,512,2]{2,1,3,0:T(8,128)S(1)}) fusion(pred[512,1024]{0,1:T(8,128)(4,1)S(1)} %copy-done.1, bf16[1024,2,128,1]{0,2,3,1:T(8,128)(2,1)S(1)} %bitcast.158, bf16[512,2,2,128]{0,3,2,1:T(8,128)(2,1)S(1)} %bitcast.163), kind=kOutput, calls=%fused_computation.10 | convolution fusion | flops 545257472 | bytes 9969664 | tf_op jit(solution)/shard_map/qkgd,ckd->kgqc/dot_general | solution.py:62
  51.3 2.8 %fusion.49 = f32[512,2,2,128]{0,3,2,1:T(8,128)S(1)} fusion(f32[512,2,2,128]{0,3,2,1:T(8,128)S(1)} %fusion.26, bf16[1024,2,128,1]{0,2,3,1:T(8,128)(2,1)S(1)} %bitcast.155, f32[2,1024,512,2]{2,1,3,0:T(8,128)S(1)} %get-tuple-element.32, pred[512,1024]{0,1:T(8,128)(4,1)S(1)} %copy-done.1), kind=kOutput, calls=%fused_computation.48 | convolution fusion | flops 545521664 | bytes 11534336 | tf_op jit(solution)/shard_map/kgqc,ckd->qkgd/dot_general | solution.py:69
  54.0 7.9 %collective-permute-done.1 = bf16[2,1024,256]{1,2,0:T(8,128)(2,1)S(1)} collective-permute-done((bf16[2,1024,256]{1,2,0:T(8,128)(2,1)}, bf16[2,1024,256]{1,2,0:T(8,128)(2,1)S(1)}, u32[]{:S(2)}, u32[]{:S(2)}) %collective-permute-start.1) | collective-permute-done | bytes 1048608 | tf_op jit(solution)/shard_map/ppermute | solution.py:19
  61.9 0.1 fusion.83
  62.0 1.9 collective-permute-start.2
  64.0 2.7 %fusion.2 = (f32[2,2,512]{2,1,0:T(2,128)S(1)}, f32[2,1024,512,2]{2,1,3,0:T(8,128)S(1)}) fusion(pred[512,1024]{0,1:T(8,128)(4,1)S(1)} %copy.38, bf16[1024,2,128,1]{0,2,3,1:T(8,128)(2,1)S(1)} %bitcast.159, bf16[512,2,2,128]{0,3,2,1:T(8,128)(2,1)S(1)} %bitcast.164), kind=kOutput, calls=%fused_computation.12 | convolution fusion | flops 545257472 | bytes 9969664 | tf_op jit(solution)/shard_map/qkgd,ckd->kgqc/dot_general | solution.py:62
  66.7 2.8 %fusion.46 = f32[512,2,2,128]{0,3,2,1:T(8,128)S(1)} fusion(f32[512,2,2,128]{0,3,2,1:T(8,128)S(1)} %fusion.49, bf16[1024,2,128,1]{0,2,3,1:T(8,128)(2,1)S(1)} %bitcast.156, f32[2,1024,512,2]{2,1,3,0:T(8,128)S(1)} %get-tuple-element.28, pred[512,1024]{0,1:T(8,128)(4,1)S(1)} %copy.38), kind=kOutput, calls=%fused_computation.47 | convolution fusion | flops 545521664 | bytes 11534336 | tf_op jit(solution)/shard_map/kgqc,ckd->qkgd/dot_general | solution.py:69
  69.5 9.6 %collective-permute-done.2 = bf16[2,1024,256]{1,2,0:T(8,128)(2,1)S(1)} collective-permute-done((bf16[2,1024,256]{1,2,0:T(8,128)(2,1)S(1)}, bf16[2,1024,256]{1,2,0:T(8,128)(2,1)S(1)}, u32[]{:S(2)}, u32[]{:S(2)}) %collective-permute-start.2) | collective-permute-done | bytes 1048608 | tf_op jit(solution)/shard_map/ppermute | solution.py:19
  79.0 0.1 fusion.82
  79.1 2.1 %collective-permute-start.3 = (bf16[2,1024,256]{1,2,0:T(8,128)(2,1)S(1)}, bf16[2,1024,256]{1,2,0:T(8,128)(2,1)S(1)}, u32[]{:S(2)}, u32[]{:S(2)}) collective-permute-start(bf16[2,1024,256]{1,2,0:T(8,128)(2,1)S(1)} %collective-permute-done.2), channel_id=1, source_target_pairs={{0,8},{8,16},{16,24},{24,32},{32,40},{40,48},{48,56},{56,64},{64,7... | collective-permute-start | bytes 3145736 | tf_op jit(solution)/shard_map/ppermute | solution.py:19
  81.3 2.8 %fusion.4 = (f32[2,2,512]{2,1,0:T(2,128)S(1)}, f32[2,1024,512,2]{2,1,3,0:T(8,128)S(1)}) fusion(pred[512,1024]{0,1:T(8,128)(4,1)S(1)} %copy.42, bf16[1024,2,128,1]{0,2,3,1:T(8,128)(2,1)S(1)} %bitcast.160, bf16[512,2,2,128]{0,3,2,1:T(8,128)(2,1)S(1)} %bitcast.165), kind=kOutput, calls=%fused_computation.14 | convolution fusion | flops 545257472 | bytes 9969664 | tf_op jit(solution)/shard_map/qkgd,ckd->kgqc/dot_general | solution.py:62
  84.1 2.8 %fusion.43 = f32[512,2,2,128]{0,3,2,1:T(8,128)S(1)} fusion(f32[512,2,2,128]{0,3,2,1:T(8,128)S(1)} %fusion.46, bf16[1024,2,128,1]{0,2,3,1:T(8,128)(2,1)S(1)} %bitcast.157, f32[2,1024,512,2]{2,1,3,0:T(8,128)S(1)} %get-tuple-element.26, pred[512,1024]{0,1:T(8,128)(4,1)S(1)} %copy.42), kind=kOutput, calls=%fused_computation.46 | convolution fusion | flops 545521664 | bytes 11534336 | tf_op jit(solution)/shard_map/kgqc,ckd->qkgd/dot_general | solution.py:69
  86.9 9.3 %collective-permute-done.3 = bf16[2,1024,256]{1,2,0:T(8,128)(2,1)S(1)} collective-permute-done((bf16[2,1024,256]{1,2,0:T(8,128)(2,1)S(1)}, bf16[2,1024,256]{1,2,0:T(8,128)(2,1)S(1)}, u32[]{:S(2)}, u32[]{:S(2)}) %collective-permute-start.3) | collective-permute-done | bytes 1048608 | tf_op jit(solution)/shard_map/ppermute | solution.py:19
  96.1 0.1 fusion.81
  96.2 0.0 slice-start
  96.2 2.7 %fusion.6 = (f32[2,2,512]{2,1,0:T(2,128)S(1)}, f32[2,1024,512,2]{2,1,3,0:T(8,128)S(1)}) fusion(pred[512,1024]{0,1:T(8,128)(4,1)S(1)} %copy.46, bf16[1024,2,128,1]{0,2,3,1:T(8,128)(2,1)S(1)} %bitcast.161, bf16[512,2,2,128]{0,3,2,1:T(8,128)(2,1)S(1)} %bitcast.166), kind=kOutput, calls=%fused_computation.16 | convolution fusion | flops 545257472 | bytes 9969664 | tf_op jit(solution)/shard_map/qkgd,ckd->kgqc/dot_general | solution.py:62
  98.9 0.0 slice-start.1
  99.0 2.8 %divide_convert_fusion = bf16[512,2,2,128]{0,3,2,1:T(8,128)(2,1)S(1)} fusion(f32[512,2,2,128]{0,3,2,1:T(8,128)S(1)} %fusion.43, bf16[1024,2,128,1]{0,2,3,1:T(8,128)(2,1)S(1)} %bitcast.154, f32[2,1024,512,2]{2,1,3,0:T(8,128)S(1)} %get-tuple-element.24, pred[512,1024]{0,1:T(8,128)(4,1)S(1)} %copy.46, f32[512,2,2]{0,2,1:T(2,128)S(1)} %add_bitcast_fusion), kind=kOutput, calls=%fused_computation.55 | convolution fusion | flops 546045952 | bytes 11018240 | tf_op jit(solution)/shard_map/kgqc,ckd->qkgd/dot_general | solution.py:69
  101.8 0.0 slice-done
  101.8 0.0 slice-done.1
  101.8 4.4 %convolution_convert_fusion = bf16[512,4608]{1,0:T(8,128)(2,1)} fusion(bf16[512,512]{0,1:T(8,128)(2,1)S(1)} %bitcast.152, bf16[512,4608]{1,0:T(8,128)(2,1)S(1)} %bitcast.148), kind=kOutput, calls=%fused_computation.9 | convolution fusion | flops 2418278400 | bytes 9961472 | tf_op jit(solution)/shard_map/dot_general | solution.py:95
  106.2 0.0 reduce-scatter.3.cloned.1.call-update
  106.2 0.0 copy-start.2
  106.2 0.0 reduce-scatter.5.cloned.1.call-start
  106.3 53.3 %reduce-scatter.3.cloned.1.call-done = bf16[128,4608]{1,0:T(8,128)(2,1)} async-done(((bf16[512,4608]{1,0:T(8,128)(2,1)}), bf16[128,4608]{1,0:T(8,128)(2,1)}) %reduce-scatter.3.cloned.1.call-update) | async-done | bytes 1179664 | tf_op jit(solution)/shard_map/reduce_scatter | solution.py:25
  159.5 0.0 reduce-scatter.5.cloned.1.call-update
  159.5 7.2 %convert_element_type.39 = f32[512,4608]{1,0:T(8,128)} convert(bf16[512,4608]{1,0:T(8,128)(2,1)} %param.9) | non-fusion elementwise | flops 2359296 | bytes 14155776 | tf_op jit(solution)/shard_map/convert_element_type | solution.py:37
  166.7 20.7 %reduce-scatter.5.cloned.1.call-done = bf16[64,4608]{1,0:T(8,128)(2,1)} async-done(((bf16[128,4608]{1,0:T(8,128)(2,1)}), bf16[64,4608]{1,0:T(8,128)(2,1)}) %reduce-scatter.5.cloned.1.call-update) | async-done | bytes 589840 | tf_op jit(solution)/shard_map/reduce_scatter | solution.py:25
  187.5 1.3 fusion.53
  188.8 0.0 copy-done.2
  188.8 2.5 %fusion.56 = bf16[64,4608]{1,0:T(8,128)(2,1)} fusion(bf16[64,4608]{1,0:T(8,128)(2,1)} %reduce-scatter.5.cloned.1.call-done, f32[512,4608]{1,0:T(8,128)} %convert_element_type.39, s32[]{:T(128)S(6)} %select_n.28, f32[4608]{0:T(1024)S(1)} %copy-done.2, f32[64]{0:T(128)S(1)} %add_rsqrt_fusion.1), kind=kLoop, calls=%fused_computation.53 | loop fusion | flops 1474560 | bytes 2377988 | tf_op jit(solution)/shard_map/convert_element_type | solution.py:103
  (7 shorter events, 0.0 us)
Async XLA Ops:
  6.5 12.9 %copy-start.3 = (s32[16]{0:T(128)S(1)}, s32[16]{0:T(128)}, u32[]{:S(2)}) copy-start(s32[16]{0:T(128)} %param.17) | copy-start | bytes 196
  6.5 23.8 %copy-start.4 = (f32[4608]{0:T(1024)S(1)}, f32[4608]{0:T(1024)}, u32[]{:S(2)}) copy-start(f32[4608]{0:T(1024)} %param.10) | copy-start | bytes 55300
  6.5 153.0 %reduce-scatter.3.cloned.1.call-start = ((), (), s32[]{:S(2)}) async-start(), calls=%async_computation.2 | async-start | bytes 5898240 | tf_op jit(solution)/shard_map/reduce_scatter | solution.py:25
  10.2 33.2 %collective-permute-start = (bf16[2,1024,256]{1,2,0:T(8,128)(2,1)}, bf16[2,1024,256]{1,2,0:T(8,128)(2,1)}, u32[]{:S(2)}, u32[]{:S(2)}) collective-permute-start(bf16[2,1024,256]{1,2,0:T(8,128)(2,1)} %pad_maximum_fusion), channel_id=1, source_target_pairs={{0,8},{8,16},{16,24},{24,32},{32,40},{40,48},{48,56},{56,64},{64,7... | collective-permute-start | bytes 3145736 | tf_op jit(solution)/shard_map/ppermute | solution.py:19
  30.4 6.6 %copy-start = (bf16[1024,2,128]{2,1,0:T(2,128)(2,1)S(1)}, bf16[1024,2,128]{2,1,0:T(2,128)(2,1)}, u32[]{:S(2)}) copy-start(bf16[1024,2,128]{2,1,0:T(2,128)(2,1)} %reshape_squeeze_stack.6) | copy-start | bytes 1572868
  40.7 7.7 %copy-start.1 = (pred[512,1024]{0,1:T(8,128)(4,1)S(1)}, pred[512,1024]{0,1:T(8,128)(4,1)}, u32[]{:S(2)}) copy-start(pred[512,1024]{0,1:T(8,128)(4,1)} %copy.34) | copy-start | bytes 1572868
  44.7 17.2 %collective-permute-start.1 = (bf16[2,1024,256]{1,2,0:T(8,128)(2,1)}, bf16[2,1024,256]{1,2,0:T(8,128)(2,1)S(1)}, u32[]{:S(2)}, u32[]{:S(2)}) collective-permute-start(bf16[2,1024,256]{1,2,0:T(8,128)(2,1)} %collective-permute-done), channel_id=1, source_target_pairs={{0,8},{8,16},{16,24},{24,32},{32,40},{40,48},{48,56},{56,64},{64,7... | collective-permute-start | bytes 3145736 | tf_op jit(solution)/shard_map/ppermute | solution.py:19
  62.0 17.0 %collective-permute-start.2 = (bf16[2,1024,256]{1,2,0:T(8,128)(2,1)S(1)}, bf16[2,1024,256]{1,2,0:T(8,128)(2,1)S(1)}, u32[]{:S(2)}, u32[]{:S(2)}) collective-permute-start(bf16[2,1024,256]{1,2,0:T(8,128)(2,1)S(1)} %collective-permute-done.1), channel_id=1, source_target_pairs={{0,8},{8,16},{16,24},{24,32},{32,40},{40,48},{48,56},{56,64},{64,7... | collective-permute-start | bytes 3145736 | tf_op jit(solution)/shard_map/ppermute | solution.py:19
  79.1 17.0 %collective-permute-start.3 = (bf16[2,1024,256]{1,2,0:T(8,128)(2,1)S(1)}, bf16[2,1024,256]{1,2,0:T(8,128)(2,1)S(1)}, u32[]{:S(2)}, u32[]{:S(2)}) collective-permute-start(bf16[2,1024,256]{1,2,0:T(8,128)(2,1)S(1)} %collective-permute-done.2), channel_id=1, source_target_pairs={{0,8},{8,16},{16,24},{24,32},{32,40},{40,48},{48,56},{56,64},{64,7... | collective-permute-start | bytes 3145736 | tf_op jit(solution)/shard_map/ppermute | solution.py:19
  96.2 5.6 %slice-start = ((s8[4718592]{0:T(1024)(128)(4,1)}), s8[4194304]{0:T(1024)(128)(4,1)S(1)}, s32[]{:S(2)}) async-start(s8[4718592]{0:T(1024)(128)(4,1)} %bitcast.147), calls=%async_computation.4 | async-start | bytes 8388608
  98.9 2.8 %slice-start.1 = ((s8[4718592]{0:T(1024)(128)(4,1)}), s8[524288]{0:T(1024)(128)(4,1)S(1)}, s32[]{:S(2)}) async-start(s8[4718592]{0:T(1024)(128)(4,1)} %bitcast.147), calls=%async_computation.5 | async-start | bytes 1048576
  106.2 82.6 %copy-start.2 = (f32[4608]{0:T(1024)S(1)}, f32[4608]{0:T(1024)}, u32[]{:S(2)}) copy-start(f32[4608]{0:T(1024)} %param.15) | copy-start | bytes 55300
  106.2 81.3 %reduce-scatter.5.cloned.1.call-start = ((), (), s32[]{:S(2)}) async-start(), calls=%async_computation.3 | async-start | bytes 1769472 | tf_op jit(solution)/shard_map/reduce_scatter | solution.py:25
Sparse Core Ops, SparseCore 0:
  106.3 53.1 reduce-scatter.2
  161.9 25.5 reduce-scatter.4
where the time goes:
time: 200 us; the launch traced here: 198 us
  waiting for transfers between devices  101 us (50%)
  matrix products  39.6 us (20%)
  other arithmetic  22.3 us (11%)
  between operations  13.8 us (7%)
  local copies, waits for them, and re-layouts  12 us (6%)
  starting transfers between devices  9.7 us (5%)
    reduce_scatter x2, waiting for transfers between devices, summed_rows(): total = lax.psum_scatter(total, axis, scatter_dimension=0, tiled=True)  74 us
    ppermute x4, waiting for transfers between devices, passed_along(): return lax.ppermute(block, axis, route)  26.7 us
    dot_general x5, matrix products, attend(): jnp.einsum('qkgd,ckd->kgqc', queries, key_block, preferred_element_type=j...  14.8 us
    dot_general x5, matrix products, attend(): jnp.einsum('kgqc,ckd->qkgd', weight.astype(jnp.bfloat16), value_block, pr...  13.9 us
    ppermute x4, starting transfers between devices, passed_along(): return lax.ppermute(block, axis, route)  9.66 us
    convert_element_type x1, other arithmetic, shards(): inputs = hidden_in.astype(jnp.float32)  7.2 us
    dot_general x1, matrix products, shards(): jnp.dot(normed, w_query, preferred_element_type=jnp.float32)  6.56 us
    dot_general x1, matrix products, shards(): jnp.dot(attended, w_out, preferred_element_type=jnp.float32)  4.36 us
  transfers between devices with their start and end apart: 6, of which 5 were waited for; matrix products, arithmetic and copies ran while one was open for 28% of the time, Pallas kernels for 0%

commit v1 on v0

v1 whole, which is shorter than its diff:
```python
import math

import jax
import jax.numpy as jnp
from jax import lax
from jax.experimental import pallas as pl
from jax.experimental.pallas import tpu as pltpu
from jax.sharding import PartitionSpec as P

MESH = pl.DeviceIdType.MESH
D = 4608
HD = 128
CTX = 1024
QR = 512
HALO = 4
CH = 128
NCH = CTX // CH
GR = 256
WCH = 16
NW = 8
NP = 6
PC = D // NP
BF = jnp.bfloat16
F32 = jnp.float32
SCALE = 144 ** (-0.5)
EXP_SCALE = 50.0 * math.log2(math.e)
TO_Z, TO_X, TO_C1, TO_C3 = range(4)
SLOT = {TO_Z: 4, TO_X: 2, TO_C1: 1, TO_C3: 3}
PIECES = (0, 3, 1, 4, 2, 5)


def layer(
    gain, post, starts, counts, hid_in, wq_in, k_in, v_in, wo_in, out,
    hid, nrm, wq, kbuf, vbuf, qbuf, acc, att, attr, wo, wp, keep, rs_s, rs_r,
    hid_sem, load_sem, kv_s, kv_r, w_s, w_r, att_s, att_r, rss_sem, rsr_sem,
):
    s = lax.axis_index("seq")
    t = lax.axis_index("tp")
    c = s % 2
    xl = (s // 2) % 2
    z = s // 4
    xh = t % 2
    y = t // 2

    def dev(z_=None, xl_=None, c_=None, y_=None, xh_=None):
        z_ = z if z_ is None else z_
        xl_ = xl if xl_ is None else xl_
        c_ = c if c_ is None else c_
        y_ = y if y_ is None else y_
        xh_ = xh if xh_ is None else xh_
        return (z_ * 4 + xl_ * 2 + c_, y_ * 2 + xh_)

    z_up = dev(z_=(z + 1) % 4)
    z_down = dev(z_=(z + 3) % 4)
    x_near = dev(xl_=1 - xl)
    core = dev(c_=1 - c)
    x_far = dev(xh_=1 - xh)
    cross = dev(xl_=1 - xl, xh_=1 - xh)
    y_up = dev(y_=(y + 1) % 4)
    y_down = dev(y_=(y + 3) % 4)

    def block_row(slot_delta):
        return ((y + slot_delta) % 4) * 128

    loads = []
    for slot, delta in enumerate((3, 1, 2, 0)):
        rows = pl.ds(pl.multiple_of(block_row(delta), 128), 128)
        loads.append(
            pltpu.make_async_copy(hid_in.at[rows, :], hid.at[pl.ds(slot * 128, 128), :], hid_sem.at[slot])
        )
    load_wq = pltpu.make_async_copy(wq_in, wq, load_sem.at[0])
    load_k = pltpu.make_async_copy(k_in, kbuf.at[0], load_sem.at[1])
    load_v = pltpu.make_async_copy(v_in, vbuf.at[0], load_sem.at[2])
    load_wo = pltpu.make_async_copy(wo_in, wo, load_sem.at[3])
    for load in loads:
        load.start()
    load_wq.start()

    barrier = pltpu.get_barrier_semaphore()
    for other in (z_up, z_down, x_near, core, x_far, cross, y_up, y_down):
        pl.semaphore_signal(barrier, inc=1, device_id=other, device_id_type=MESH)
    pl.semaphore_wait(barrier, 8)

    def remote(src, dst, send, recv, to):
        return pltpu.make_async_remote_copy(
            src_ref=src, dst_ref=dst, send_sem=send, recv_sem=recv, device_id=to, device_id_type=MESH
        )

    kv_to = {TO_Z: z_up, TO_X: x_near, TO_C1: core, TO_C3: core}

    def kv_copies(stream, j, src):
        slot = SLOT[stream]
        rows = pl.ds(j * CH, CH)
        k_src = k_in.at[rows, :] if src is None else kbuf.at[src, rows, :]
        v_src = v_in.at[rows, :] if src is None else vbuf.at[src, rows, :]
        return (
            remote(k_src, kbuf.at[slot, rows, :], kv_s.at[stream, j, 0], kv_r.at[stream, j, 0], kv_to[stream]),
            remote(v_src, vbuf.at[slot, rows, :], kv_s.at[stream, j, 1], kv_r.at[stream, j, 1], kv_to[stream]),
        )

    def kv_send(stream, j, src):
        for copy in kv_copies(stream, j, src):
            copy.start()

    def kv_wait(stream, j):
        for copy in kv_copies(stream, j, SLOT[stream]):
            copy.wait_recv()

    parity = z % 2
    W_CROSS, W_DOWN, W_CA, W_CB = range(4)
    w_to = {W_CROSS: cross, W_DOWN: z_down, W_CA: core, W_CB: core}

    def w_copy(stream, j, quarter, from_input=False):
        rows = pl.ds(pl.multiple_of(quarter * 128 + j * WCH, WCH), WCH)
        src = wo_in.at[rows, :] if from_input else wp.at[rows, :]
        return remote(src, wp.at[rows, :], w_s.at[stream, j], w_r.at[stream, j], w_to[stream])

    mine = parity * 2 + c
    above = (1 - parity) * 2 + c
    w_arrives = {
        W_CROSS: mine,
        W_DOWN: above,
        W_CA: parity * 2 + (1 - c),
        W_CB: (1 - parity) * 2 + (1 - c),
    }

    for j in range(NCH):
        kv_send(TO_Z, j, None)

        @pl.when(xl == 0)
        def _():
            kv_send(TO_X, j, None)

        @pl.when(c == 0)
        def _():
            kv_send(TO_C1, j, None)

        w_copy(W_CROSS, j, mine, from_input=True).start()
    load_k.start()
    load_v.start()
    load_wo.start()

    def step_f(j):
        kv_wait(TO_Z, j)

        @pl.when(xl == 1)
        def _():
            kv_send(TO_X, j, 4)

        @pl.when(c == 1)
        def _():
            kv_send(TO_C3, j, 4)

    def step_g(j):
        kv_wait(TO_X, j)

        @pl.when(c == 0)
        def _():
            kv_send(TO_C3, j, 2)

        @pl.when(c == 1)
        def _():
            kv_send(TO_C1, j, 2)

    def step_e(j):
        kv_wait(TO_C1, j)
        kv_wait(TO_C3, j)

    def step_w(j):
        w_copy(W_CROSS, j, mine).wait_recv()
        w_copy(W_DOWN, j, mine).start()
        w_copy(W_CA, j, mine).start()

    def step_z(j):
        w_copy(W_DOWN, j, above).wait_recv()
        w_copy(W_CB, j, above).start()

    def norm_rows(i, carry):
        rows = pl.ds(pl.multiple_of(i * 16, 16), 16)
        x = hid[rows, :].astype(F32)
        r = lax.rsqrt(jnp.mean(x * x, axis=-1, keepdims=True) + 0.1)
        nrm[rows, :] = (x * r * gain[...]).astype(BF)
        return carry

    for slot in range(4):
        loads[slot].wait()
        lax.fori_loop(slot * 8, slot * 8 + 8, norm_rows, 0)
    step_f(0)
    step_w(0)
    load_wq.wait()
    for kh in range(2):
        q = jnp.dot(nrm[...], wq[:, kh * 256 : kh * 256 + 256], preferred_element_type=F32)
        q = (q * SCALE).astype(BF)
        for slot in range(4):
            for g in range(2):
                qbuf[kh, slot * 256 + g * 128 : slot * 256 + g * 128 + 128, :] = q[
                    slot * 128 : slot * 128 + 128, g * 128 : g * 128 + 128
                ]
    acc[...] = jnp.zeros_like(acc)

    off = starts[s] - s * CTX
    filled = {}
    for d in range(1, HALO + 1):
        source = s - d
        filled[d] = jnp.where(source >= 0, counts[jnp.maximum(source, 0)], 0)

    def attend(base, kh, tile):
        lanes = pl.ds(pl.multiple_of(kh * HD, HD), HD)
        rows = pl.ds(pl.multiple_of(tile * 512, 512), 512)
        q = qbuf[kh, rows, :]
        row_ids = lax.broadcasted_iota(jnp.int32, (GR, HD), 0)

        def scores(d):
            key = kbuf[d, base : base + GR, lanes]
            return lax.dot_general(q, key, (((1,), (1,)), ((), ())), preferred_element_type=F32)

        def weights(x):
            return jnp.exp2(jnp.tanh(x * (1.0 / 50.0)) * EXP_SCALE)

        def values(d):
            v = vbuf[d, base : base + GR, lanes]
            if d == 0:
                return jnp.concatenate([v, jnp.ones_like(v)], axis=1)
            keep_row = jnp.where(row_ids < filled[d] - base, 1.0, 0.0).astype(BF)
            return jnp.concatenate([v * keep_row, keep_row], axis=1)

        total = None
        for d in (1, 2, 3):
            w = weights(scores(d)).astype(BF)
            part = jnp.dot(w, values(d), preferred_element_type=F32)
            total = part if total is None else total + part
        near, far = scores(0), scores(4)
        pattern = lax.broadcasted_iota(jnp.int32, (128, GR), 1) - lax.broadcasted_iota(jnp.int32, (128, GR), 0)
        w_near, w_far = [], []
        for u in range(4):
            limit = off + block_row(3 - 2 * (u // 2) - tile) - base
            is_near = pattern <= limit
            part_rows = slice(u * 128, u * 128 + 128)
            w = weights(jnp.where(is_near, near[part_rows], far[part_rows]))
            w_near.append(jnp.where(is_near, w, 0.0).astype(BF))
            w_far.append(jnp.where(is_near, 0.0, w).astype(BF))
        total = total + jnp.dot(jnp.concatenate(w_near, axis=0), values(0), preferred_element_type=F32)
        total = total + jnp.dot(jnp.concatenate(w_far, axis=0), values(4), preferred_element_type=F32)
        acc[kh, rows, :] += total

    def attend_tiles(base, kh):
        def body(tile, carry):
            attend(base, kh, tile)
            return carry

        lax.fori_loop(0, 2, body, 0)

    step_f(1)
    step_w(1)
    step_g(0)
    step_f(2)
    step_w(2)
    load_k.wait()
    load_v.wait()
    step_g(1)
    step_e(0)
    step_e(1)
    attend_tiles(0, 0)
    step_f(3)
    step_w(3)
    step_z(0)
    attend_tiles(0, 1)
    step_f(4)
    step_w(4)
    step_z(1)
    step_g(2)
    step_f(5)
    step_w(5)
    step_g(3)
    step_e(2)
    step_e(3)
    attend_tiles(256, 0)
    step_f(6)
    step_w(6)
    step_z(2)
    attend_tiles(256, 1)
    step_g(4)
    step_f(7)
    step_w(7)
    step_z(3)
    step_z(4)
    step_g(5)
    step_e(4)
    step_e(5)
    attend_tiles(512, 0)
    step_g(6)
    step_z(5)
    attend_tiles(512, 1)
    step_g(7)
    step_e(6)
    step_e(7)

    def att_copy(slot):
        rows = pl.ds(pl.multiple_of((1 - xh) * 64, 64), 64)
        return remote(att.at[slot, rows, :], attr.at[slot], att_s.at[slot], att_r.at[slot], x_far)

    for tile in range(2):
        def body(kh, carry):
            attend(768, kh, tile)
            return carry

        lax.fori_loop(0, 2, body, 0)
        for kh in range(2):
            a = acc[kh, tile * 512 : tile * 512 + 512, :]
            o = (a[:, :HD] / a[:, HD:]).astype(BF)
            for u in range(4):
                head = kh * 2 + u % 2
                att[2 * tile + u // 2, :, head * HD : head * HD + HD] = o[u * 128 : u * 128 + 128, :]
        for slot in (2 * tile, 2 * tile + 1):
            att_copy(slot).start()
        step_z(6 + tile)

    for j in range(NW):
        w_copy(W_CA, j, w_arrives[W_CA]).wait_recv()
        w_copy(W_CB, j, w_arrives[W_CB]).wait_recv()
    load_wo.wait()

    def rs_copy(step, p):
        to = y_up if p < NP // 2 else y_down
        return remote(rs_s.at[step, p], rs_r.at[step, p], rss_sem.at[step, p], rsr_sem.at[step, p], to)

    own_rows = pl.ds(pl.multiple_of(xh * 64, 64), 64)
    for tile in range(2):
        for slot in (2 * tile, 2 * tile + 1):
            att_copy(slot).wait_recv()
        lhs = jnp.concatenate([att[2 * tile, own_rows, :], att[2 * tile + 1, own_rows, :]], axis=0)
        lhs_far = jnp.concatenate([attr[2 * tile], attr[2 * tile + 1]], axis=0)
        for p in PIECES:
            cols = slice(p * PC, p * PC + PC)
            r = jnp.dot(lhs, wo[:, cols], preferred_element_type=F32)
            r = r + jnp.dot(lhs_far, wp[:, cols], preferred_element_type=F32)
            if tile == 0:
                first, later = (r[:64], r[64:]) if p < NP // 2 else (r[64:], r[:64])
                rs_s[0, p] = first.astype(BF)
                rs_copy(0, p).start()
                keep[1, :, cols] = later
            else:
                keep[0, :, cols] = r[:64]
                keep[2, :, cols] = r[64:]
    for step in (1, 2):
        for p in PIECES:
            cols = slice(p * PC, p * PC + PC)
            rs_copy(step - 1, p).wait_recv()
            rs_s[step, p] = (rs_r[step - 1, p].astype(F32) + keep[step - 1, :, cols]).astype(BF)
            rs_copy(step, p).start()
    squares = jnp.zeros((64, 1), F32)
    for p in PIECES:
        cols = slice(p * PC, p * PC + PC)
        rs_copy(2, p).wait_recv()
        part = rs_r[2, p].astype(F32) + keep[2, :, cols]
        keep[2, :, cols] = part
        squares = squares + jnp.sum(part * part, axis=-1, keepdims=True)
    factor = lax.rsqrt(squares * (1.0 / D) + 0.1)
    residual_rows = pl.ds(pl.multiple_of(384 + xh * 64, 64), 64)
    for p in range(NP):
        cols = slice(p * PC, p * PC + PC)
        residual = hid[residual_rows, cols].astype(F32)
        out[:, cols] = (residual + keep[2, :, cols] * factor * post[:, cols]).astype(BF)

    for j in range(NCH):
        for stream in (TO_Z, TO_X, TO_C1, TO_C3):
            for copy in kv_copies(stream, j, SLOT[stream]):
                copy.wait_send()
    for j in range(NW):
        for stream in (W_CROSS, W_DOWN, W_CA, W_CB):
            w_copy(stream, j, mine).wait_send()
    for slot in range(4):
        att_copy(slot).wait_send()
    for step in range(3):
        for p in PIECES:
            rs_copy(step, p).wait_send()


def shards(hidden_in, pre_gain, w_query, key_cache, value_cache, w_out, post_gain, starts, counts):
    vmem = pl.BlockSpec(memory_space=pltpu.VMEM)
    smem = pl.BlockSpec(memory_space=pltpu.SMEM)
    hbm = pl.BlockSpec(memory_space=pl.ANY)
    dma = pltpu.SemaphoreType.DMA
    return pl.pallas_call(
        layer,
        out_shape=jax.ShapeDtypeStruct((64, D), BF),
        in_specs=[vmem, vmem, smem, smem, hbm, hbm, hbm, hbm, hbm],
        out_specs=vmem,
        scratch_shapes=[
            pltpu.VMEM((QR, D), BF),
            pltpu.VMEM((QR, D), BF),
            pltpu.VMEM((D, 512), BF),
            pltpu.VMEM((HALO + 1, CTX, 256), BF),
            pltpu.VMEM((HALO + 1, CTX, 256), BF),
            pltpu.VMEM((2, 1024, HD), BF),
            pltpu.VMEM((2, 1024, 256), F32),
            pltpu.VMEM((4, 128, 512), BF),
            pltpu.VMEM((4, 64, 512), BF),
            pltpu.VMEM((512, D), BF),
            pltpu.VMEM((512, D), BF),
            pltpu.VMEM((3, 64, D), F32),
            pltpu.VMEM((3, NP, 64, PC), BF),
            pltpu.VMEM((3, NP, 64, PC), BF),
            dma((4,)),
            dma((4,)),
            dma((4, NCH, 2)),
            dma((4, NCH, 2)),
            dma((4, NW)),
            dma((4, NW)),
            dma((4,)),
            dma((4,)),
            dma((3, NP)),
            dma((3, NP)),
        ],
        compiler_params=pltpu.CompilerParams(
            collective_id=0, has_side_effects=True, vmem_limit_bytes=60 * 1024 * 1024
        ),
        name="layer",
    )(
        pre_gain.reshape(1, D), post_gain.reshape(1, D), starts, counts,
        hidden_in, w_query, key_cache, value_cache, w_out,
    )


def solution(mesh):
    in_specs = (
        P("seq", None),
        P(),
        P(None, "tp"),
        P("seq", "tp"),
        P("seq", "tp"),
        P("tp", None),
        P(),
        P(),
        P(),
    )
    return jax.shard_map(
        shards, mesh=mesh, in_specs=in_specs, out_specs=P(("seq", "tp"), None), check_vma=False
    )
```

time: 200 us -> 81.4 us (0.41)
  the two profiles are of different devices: /device:TPU:32 before, /device:TPU:1 now
where the time goes in v1:
time: 81.4 us; the launch traced here: 81.1 us
  Pallas kernels  76.5 us (94%)
  local copies, waits for them, and re-layouts  4.6 us (6%)
    pallas_call x1, Pallas kernels, shards(): pl.pallas_call(layer, out_shape=jax.ShapeDtypeStruct((64, D), BF), in_spe...  76.5 us
    unnamed x1, local copies, waits for them, and re-layouts  1.92 us

profile of v1, /device:TPU:1, one launch (start us, length us, event | category | flops | bytes accessed | tf_op | source)
XLA Modules:
  0.0 81.1 jit_solution(16329092921988670191)
XLA Ops:
  0.0 1.3 %reshape.6.gain = f32[1,4608]{1,0:T(1,128)} reshape(f32[4608]{0:T(1024)} %param.10) | data formatting | bytes 36864 | tf_op jit(solution)/shard_map/reshape | solution.py:420
  1.3 1.3 %reshape.7.post = f32[1,4608]{1,0:T(1,128)} reshape(f32[4608]{0:T(1024)} %param.15) | data formatting | bytes 36864 | tf_op jit(solution)/shard_map/reshape | solution.py:420
  2.7 76.5 %layer.1 = bf16[64,4608]{1,0:T(8,128)(2,1)} custom-call(f32[1,4608]{1,0:T(1,128)} %reshape.6.gain, f32[1,4608]{1,0:T(1,128)} %reshape.7.post, s32[16]{0:T(128)} %starts.1, s32[16]{0:T(128)} %counts.1, bf16[512,4608]{1,0:T(8,128)(2,1)} %hid_in.1, bf16[4608,512]{1,0:T(8,128)(2,1)} %wq_in.1, bf16[1024,256]{1,0:T(8,128)(2,1)} %k_in.1, bf16[1024,256]{1,0:T(8,128)(2,1)} %v_in.1, ...), custom_call_target="tpu_custom_call" | custom-call | tf_op jit(solution)/shard_map/layer/pallas_call | solution.py:384
  79.2 1.9 %copy.11 = bf16[64,4608]{1,0:T(8,128)(2,1)} copy(bf16[64,4608]{1,0:T(8,128)(2,1)} %layer.1) | data formatting | bytes 1179648

commit v2 on v1

v2 whole, which is shorter than its diff:
```python
import math

import jax
import jax.numpy as jnp
from jax import lax
from jax.experimental import pallas as pl
from jax.experimental.pallas import tpu as pltpu
from jax.sharding import PartitionSpec as P

MESH = pl.DeviceIdType.MESH
D = 4608
HD = 128
CTX = 1024
QR = 512
HALO = 4
CH = 64
NCH = CTX // CH
GR = 256
NP = 6
PC = D // NP
BF = jnp.bfloat16
F32 = jnp.float32
SCALE = 144 ** (-0.5)
EXP_SCALE = 50.0 * math.log2(math.e)
TO_Z, TO_X, TO_C1, TO_C3 = range(4)
SLOT = {TO_Z: 4, TO_X: 2, TO_C1: 1, TO_C3: 3}
PIECES = (0, 3, 1, 4, 2, 5)


def layer(
    gain_in, post_in, starts_in, counts_in, hid_in, wq_in, k_in, v_in, wo_in, out,
    gain, post, starts, counts, hid, nrm, wq, kbuf, vbuf, qbuf, acc, att, attr, wo, wp, part, rs_s, rs_r, obuf,
    hid_sem, load_sem, kv_s, kv_r, w_s, w_r, att_s, att_r, rss_sem, rsr_sem,
):
    s = lax.axis_index("seq")
    t = lax.axis_index("tp")
    c = s % 2
    xl = (s // 2) % 2
    z = s // 4
    xh = t % 2
    y = t // 2

    def dev(z_=None, xl_=None, c_=None, y_=None, xh_=None):
        z_ = z if z_ is None else z_
        xl_ = xl if xl_ is None else xl_
        c_ = c if c_ is None else c_
        y_ = y if y_ is None else y_
        xh_ = xh if xh_ is None else xh_
        return (z_ * 4 + xl_ * 2 + c_, y_ * 2 + xh_)

    z_up = dev(z_=(z + 1) % 4)
    z_down = dev(z_=(z + 3) % 4)
    x_near = dev(xl_=1 - xl)
    core = dev(c_=1 - c)
    x_far = dev(xh_=1 - xh)
    cross = dev(xl_=1 - xl, xh_=1 - xh)
    y_up = dev(y_=(y + 1) % 4)
    y_down = dev(y_=(y + 3) % 4)

    def block_row(slot_delta):
        return ((y + slot_delta) % 4) * 128

    loads = []
    for slot, delta in enumerate((3, 1, 2, 0)):
        rows = pl.ds(pl.multiple_of(block_row(delta), 128), 128)
        loads.append(
            pltpu.make_async_copy(hid_in.at[rows, :], hid.at[pl.ds(slot * 128, 128), :], hid_sem.at[slot])
        )
    load_wq = pltpu.make_async_copy(wq_in, wq, load_sem.at[0])
    load_k = pltpu.make_async_copy(k_in, kbuf.at[0], load_sem.at[1])
    load_v = pltpu.make_async_copy(v_in, vbuf.at[0], load_sem.at[2])
    load_wo = pltpu.make_async_copy(wo_in, wo, load_sem.at[3])
    load_gain = pltpu.make_async_copy(gain_in, gain, load_sem.at[4])
    small = [
        pltpu.make_async_copy(post_in, post, load_sem.at[5]),
        pltpu.make_async_copy(starts_in, starts, load_sem.at[6]),
        pltpu.make_async_copy(counts_in, counts, load_sem.at[7]),
    ]
    load_gain.start()
    for load in loads:
        load.start()
    load_wq.start()
    for load in small:
        load.start()

    barrier = pltpu.get_barrier_semaphore()
    for other in (z_up, z_down, x_near, core, x_far, cross, y_up, y_down):
        pl.semaphore_signal(barrier, inc=1, device_id=other, device_id_type=MESH)
    pl.semaphore_wait(barrier, 8)

    def remote(src, dst, send, recv, to):
        return pltpu.make_async_remote_copy(
            src_ref=src, dst_ref=dst, send_sem=send, recv_sem=recv, device_id=to, device_id_type=MESH
        )

    kv_to = {TO_Z: z_up, TO_X: x_near, TO_C1: core, TO_C3: core}

    GROUPED = (TO_C1, TO_C3)
    FIRST_SEM = {TO_Z: 0, TO_X: NCH, TO_C1: 2 * NCH, TO_C3: 2 * NCH + NCH // 4}

    def kv_send(stream, j, src):
        slot = SLOT[stream]
        rows = pl.ds(j * CH, CH)
        arrived = kv_r.at[FIRST_SEM[stream] + (j // 4 if stream in GROUPED else j)]
        for whole, buf in ((k_in, kbuf), (v_in, vbuf)):
            source = whole.at[rows, :] if src is None else buf.at[src, rows, :]
            remote(source, buf.at[slot, rows, :], kv_s.at[stream], arrived, kv_to[stream]).start()

    def kv_wait(stream, j):
        ref = kbuf.at[SLOT[stream], pl.ds(0, 8 * CH if stream in GROUPED else 2 * CH), :]
        remote(ref, ref, kv_s.at[stream], kv_r.at[FIRST_SEM[stream] + j], kv_to[stream]).wait_recv()

    def kv_sent(stream):
        ref = kbuf.at[pl.ds(0, 2)]
        remote(ref, ref, kv_s.at[stream], kv_r.at[FIRST_SEM[stream]], kv_to[stream]).wait_send()

    parity = z % 2
    W_CROSS, W_DOWN, W_CA, W_CB = range(4)
    w_to = {W_CROSS: cross, W_DOWN: z_down, W_CA: core, W_CB: core}

    def w_copy(stream, j, quarter, from_input=False):
        rows = pl.ds(pl.multiple_of(quarter * 128, 128), 128)
        cols = pl.ds(PIECES[j] * PC, PC)
        src = wo_in.at[rows, cols] if from_input else wp.at[rows, cols]
        return remote(src, wp.at[rows, cols], w_s.at[stream], w_r.at[stream, j], w_to[stream])

    def w_sent(stream):
        ref = wp.at[pl.ds(0, 128), :]
        remote(ref, ref, w_s.at[stream], w_r.at[stream, 0], w_to[stream]).wait_send()

    mine = parity * 2 + c
    above = (1 - parity) * 2 + c
    w_arrives = {
        W_CROSS: mine,
        W_DOWN: above,
        W_CA: parity * 2 + (1 - c),
        W_CB: (1 - parity) * 2 + (1 - c),
    }

    for j in range(NCH):
        kv_send(TO_Z, j, None)

        @pl.when(xl == 0)
        def _():
            kv_send(TO_X, j, None)

        @pl.when(c == 0)
        def _():
            kv_send(TO_C1, j, None)

        if j < NP:
            w_copy(W_CROSS, j, mine, from_input=True).start()
    load_k.start()
    load_v.start()
    load_wo.start()

    def step_f(j):
        kv_wait(TO_Z, j)

        @pl.when(xl == 1)
        def _():
            kv_send(TO_X, j, 4)

        @pl.when(c == 1)
        def _():
            kv_send(TO_C3, j, 4)

    def step_g(j):
        kv_wait(TO_X, j)

        @pl.when(c == 0)
        def _():
            kv_send(TO_C3, j, 2)

        @pl.when(c == 1)
        def _():
            kv_send(TO_C1, j, 2)

    def step_e(j):
        if j % 4 == 3:
            kv_wait(TO_C1, j // 4)
            kv_wait(TO_C3, j // 4)

    def step_w(j):
        w_copy(W_CROSS, j, mine).wait_recv()
        w_copy(W_DOWN, j, mine).start()
        w_copy(W_CA, j, mine).start()

    def step_z(j):
        w_copy(W_DOWN, j, above).wait_recv()
        w_copy(W_CB, j, above).start()

    def norm_rows(i, carry):
        rows = pl.ds(pl.multiple_of(i * 16, 16), 16)
        x = hid[rows, :].astype(F32)
        r = lax.rsqrt(jnp.mean(x * x, axis=-1, keepdims=True) + 0.1)
        nrm[rows, :] = (x * r * gain[...].reshape(1, D)).astype(BF)
        return carry

    done = dict.fromkeys((step_f, step_g, step_e, step_w, step_z), 0)

    def upto(step, n):
        for j in range(done[step], n):
            step(j)
        done[step] = max(done[step], n)

    load_gain.wait()
    for slot in range(4):
        loads[slot].wait()
        lax.fori_loop(slot * 8, slot * 8 + 8, norm_rows, 0, unroll=4)
    load_wq.wait()
    for m in range(2):
        q = jnp.dot(nrm[m * 256 : m * 256 + 256, :], wq[...], preferred_element_type=F32)
        q = (q * SCALE).astype(BF)
        for u in range(2):
            slot = 2 * m + u
            for kh in range(2):
                for g in range(2):
                    head = 2 * kh + g
                    qbuf[kh, slot * 256 + g * 128 : slot * 256 + g * 128 + 128, :] = q[
                        u * 128 : u * 128 + 128, head * HD : head * HD + HD
                    ]
    acc[...] = jnp.zeros_like(acc)
    for load in small:
        load.wait()
    load_k.wait()
    load_v.wait()

    off = starts[s] - s * CTX
    filled = {}
    for d in range(1, HALO + 1):
        source = s - d
        filled[d] = jnp.where(source >= 0, counts[jnp.maximum(source, 0)], 0)

    def attend(base, kh, tile, sources=(1, 2, 3, 0)):
        lanes = slice(kh * HD, kh * HD + HD)
        rows = slice(tile * 512, tile * 512 + 512)
        q = qbuf[kh, rows, :]
        row_ids = lax.broadcasted_iota(jnp.int32, (GR, HD), 0)

        def scores(d):
            key = kbuf[d, base : base + GR, lanes]
            return lax.dot_general(q, key, (((1,), (1,)), ((), ())), preferred_element_type=F32)

        def weights(x):
            return jnp.exp2(jnp.tanh(x * (1.0 / 50.0)) * EXP_SCALE)

        def values(d):
            v = vbuf[d, base : base + GR, lanes]
            if d == 0:
                return jnp.concatenate([v, jnp.ones_like(v)], axis=1)
            keep_row = jnp.where(row_ids < filled[d] - base, 1.0, 0.0).astype(BF)
            return jnp.concatenate([v * keep_row, keep_row], axis=1)

        pattern = lax.broadcasted_iota(jnp.int32, (128, GR), 1) - lax.broadcasted_iota(jnp.int32, (128, GR), 0)
        total = None
        for d in sources:
            if d == 0:
                near, far = scores(0), scores(4)
                w_near, w_far = [], []
                for u in range(4):
                    limit = off + block_row((3, 1, 2, 0)[2 * tile + u // 2]) - base
                    is_near = pattern <= limit
                    part_rows = slice(u * 128, u * 128 + 128)
                    w = weights(jnp.where(is_near, near[part_rows], far[part_rows]))
                    w_near.append(jnp.where(is_near, w, 0.0).astype(BF))
                    w_far.append(jnp.where(is_near, 0.0, w).astype(BF))
                term = jnp.dot(jnp.concatenate(w_near, axis=0), values(0), preferred_element_type=F32)
                term = term + jnp.dot(jnp.concatenate(w_far, axis=0), values(4), preferred_element_type=F32)
            else:
                term = jnp.dot(weights(scores(d)).astype(BF), values(d), preferred_element_type=F32)
            total = term if total is None else total + term
        acc[kh, rows, :] += total

    def units(base, tile, sources=(1, 2, 3, 0)):
        for kh in range(2):
            attend(base, kh, tile, sources)

    upto(step_f, 2)
    upto(step_w, 1)
    upto(step_f, 4)
    upto(step_g, 1)
    upto(step_f, 5)
    upto(step_g, 2)
    upto(step_f, 6)
    upto(step_w, 2)
    upto(step_g, 4)
    upto(step_f, 7)
    upto(step_e, 4)
    units(0, 0)
    upto(step_f, 9)
    upto(step_g, 5)
    upto(step_z, 1)
    units(0, 1)
    upto(step_w, 3)
    upto(step_f, 10)
    upto(step_g, 7)
    upto(step_f, 11)
    upto(step_g, 8)
    upto(step_z, 2)
    upto(step_e, 8)
    units(256, 0)
    upto(step_f, 13)
    upto(step_w, 4)
    upto(step_g, 10)
    units(256, 1)
    upto(step_f, 14)
    upto(step_g, 11)
    upto(step_z, 3)
    upto(step_f, 15)
    upto(step_g, 12)
    upto(step_w, 5)
    upto(step_e, 12)
    units(512, 0)
    upto(step_f, 16)
    upto(step_g, 14)
    units(512, 1)
    upto(step_w, 6)
    upto(step_z, 4)
    upto(step_g, 15)
    units(768, 0, (0,))
    upto(step_g, 16)
    units(768, 1, (0, 2))
    upto(step_e, 16)

    def att_copy(slot, kh):
        rows = pl.ds(pl.multiple_of((1 - xh) * 64, 64), 64)
        cols = pl.ds(kh * 256, 256)
        return remote(
            att.at[slot, rows, cols], attr.at[slot, :, cols], att_s, att_r.at[slot, kh], x_far
        )

    def finish(kh, tile):
        a = acc[kh, tile * 512 : tile * 512 + 512, :]
        o = (a[:, :HD] / a[:, HD:]).astype(BF)
        for u in range(4):
            head = kh * 2 + u % 2
            att[2 * tile + u // 2, :, head * HD : head * HD + HD] = o[u * 128 : u * 128 + 128, :]
        for slot in (2 * tile, 2 * tile + 1):
            att_copy(slot, kh).start()

    attend(768, 0, 0, (1, 2, 3))
    finish(0, 0)
    attend(768, 1, 0, (1, 2, 3))
    finish(1, 0)
    upto(step_z, 5)
    units(768, 1, (1, 3))
    finish(0, 1)
    finish(1, 1)

    def rs_copy(step, p):
        to = y_up if p < NP // 2 else y_down
        return remote(rs_s.at[step, p], rs_r.at[step, p], rss_sem.at[0 if p < NP // 2 else 1], rsr_sem.at[step, p], to)

    own_rows = pl.ds(pl.multiple_of(xh * 64, 64), 64)
    load_wo.wait()
    lhs = jnp.concatenate([att[slot, own_rows, :] for slot in range(4)], axis=0)
    for p in PIECES:
        cols = slice(p * PC, p * PC + PC)
        r = jnp.dot(lhs, wo[:, cols], preferred_element_type=F32)
        for slot in range(4):
            part[slot, :, cols] = r[slot * 64 : slot * 64 + 64]
    for tile in range(2):
        for slot in (2 * tile, 2 * tile + 1):
            for kh in range(2):
                att_copy(slot, kh).wait_recv()
        lhs_far = jnp.concatenate([attr[2 * tile], attr[2 * tile + 1]], axis=0)
        for j, p in enumerate(PIECES):
            if tile == 0:
                upto(step_z, j + 1)
                w_copy(W_CA, j, w_arrives[W_CA]).wait_recv()
                w_copy(W_CB, j, w_arrives[W_CB]).wait_recv()
            cols = slice(p * PC, p * PC + PC)
            r = jnp.dot(lhs_far, wp[:, cols], preferred_element_type=F32)
            if tile == 0:
                first, later = (0, 1) if p < NP // 2 else (1, 0)
                rs_s[0, p] = (part[first, :, cols] + r[first * 64 : first * 64 + 64]).astype(BF)
                rs_copy(0, p).start()
                part[later, :, cols] += r[later * 64 : later * 64 + 64]
            else:
                part[2, :, cols] += r[:64]
                part[3, :, cols] += r[64:]

    for step in (1, 2):
        for p in PIECES:
            cols = slice(p * PC, p * PC + PC)
            mine_slot = 2 if step == 1 else (1 if p < NP // 2 else 0)
            rs_copy(step - 1, p).wait_recv()
            rs_s[step, p] = (rs_r[step - 1, p].astype(F32) + part[mine_slot, :, cols]).astype(BF)
            rs_copy(step, p).start()
    squares = jnp.zeros((64, 1), F32)
    for p in PIECES:
        cols = slice(p * PC, p * PC + PC)
        rs_copy(2, p).wait_recv()
        whole = rs_r[2, p].astype(F32) + part[3, :, cols]
        part[3, :, cols] = whole
        squares = squares + jnp.sum(whole * whole, axis=-1, keepdims=True)
    factor = lax.rsqrt(squares * (1.0 / D) + 0.1)
    residual_rows = pl.ds(pl.multiple_of(384 + xh * 64, 64), 64)
    stores = []
    for p in range(NP):
        cols = slice(p * PC, p * PC + PC)
        residual = hid[residual_rows, cols].astype(F32)
        obuf[:, cols] = (residual + part[3, :, cols] * factor * post[cols].reshape(1, PC)).astype(BF)
    stores.append(pltpu.make_async_copy(obuf, out, load_sem.at[0]))
    for store in stores:
        store.start()
    for stream in (TO_Z, TO_X, TO_C1, TO_C3):
        kv_sent(stream)
    for stream in (W_CROSS, W_DOWN, W_CA, W_CB):
        w_sent(stream)
    remote(attr, attr, att_s, att_r.at[0, 0], x_far).wait_send()
    half = rs_s.at[:, pl.ds(0, NP // 2)]
    remote(half, half, rss_sem.at[0], rsr_sem.at[0, 0], y_up).wait_send()
    remote(half, half, rss_sem.at[1], rsr_sem.at[0, 0], y_down).wait_send()
    for store in stores:
        store.wait()


def shards(hidden_in, pre_gain, w_query, key_cache, value_cache, w_out, post_gain, starts, counts):
    hbm = pl.BlockSpec(memory_space=pltpu.HBM)
    dma = pltpu.SemaphoreType.DMA
    return pl.pallas_call(
        layer,
        out_shape=jax.ShapeDtypeStruct((64, D), BF),
        in_specs=[hbm] * 9,
        out_specs=hbm,
        scratch_shapes=[
            pltpu.VMEM((D,), F32),
            pltpu.VMEM((D,), F32),
            pltpu.SMEM((16,), jnp.int32),
            pltpu.SMEM((16,), jnp.int32),
            pltpu.VMEM((QR, D), BF),
            pltpu.VMEM((QR, D), BF),
            pltpu.VMEM((D, 512), BF),
            pltpu.VMEM((HALO + 1, CTX, 256), BF),
            pltpu.VMEM((HALO + 1, CTX, 256), BF),
            pltpu.VMEM((2, 1024, HD), BF),
            pltpu.VMEM((2, 1024, 256), F32),
            pltpu.VMEM((4, 128, 512), BF),
            pltpu.VMEM((4, 64, 512), BF),
            pltpu.VMEM((512, D), BF),
            pltpu.VMEM((512, D), BF),
            pltpu.VMEM((4, 64, D), F32),
            pltpu.VMEM((3, NP, 64, PC), BF),
            pltpu.VMEM((3, NP, 64, PC), BF),
            pltpu.VMEM((64, D), BF),
            dma((4,)),
            dma((8,)),
            dma((4,)),
            dma((2 * NCH + NCH // 2,)),
            dma((4,)),
            dma((4, NP)),
            dma,
            dma((4, 2)),
            dma((2,)),
            dma((3, NP)),
        ],
        compiler_params=pltpu.CompilerParams(
            collective_id=0, has_side_effects=True, vmem_limit_bytes=60 * 1024 * 1024
        ),
        name="layer",
    )(
        pre_gain, post_gain, starts, counts,
        hidden_in, w_query, key_cache, value_cache, w_out,
    )


def solution(mesh):
    in_specs = (
        P("seq", None),
        P(),
        P(None, "tp"),
        P("seq", "tp"),
        P("seq", "tp"),
        P("tp", None),
        P(),
        P(),
        P(),
    )
    return jax.shard_map(
        shards, mesh=mesh, in_specs=in_specs, out_specs=P(("seq", "tp"), None), check_vma=False
    )
```

time: 81.4 us -> 70.5 us (0.87)
  the two profiles are of different devices: /device:TPU:1 before, /device:TPU:0 now
where the time goes in v2:
time: 70.5 us; the launch traced here: 70.3 us
  Pallas kernels  68.4 us (97%)
  local copies, waits for them, and re-layouts  1.92 us (3%)
    pallas_call x1, Pallas kernels, shards(): pl.pallas_call(layer, out_shape=jax.ShapeDtypeStruct((64, D), BF), in_spe...  68.4 us
    unnamed x1, local copies, waits for them, and re-layouts  1.92 us

profile of v2, /device:TPU:0, one launch (start us, length us, event | category | flops | bytes accessed | tf_op | source)
XLA Modules:
  0.0 70.3 jit_solution(6665678812037334671)
XLA Ops:
  0.0 68.4 %layer.1 = bf16[64,4608]{1,0:T(8,128)(2,1)} custom-call(f32[4608]{0:T(1024)} %gain_in.1, f32[4608]{0:T(1024)} %post_in.1, s32[16]{0:T(128)} %starts_in.1, s32[16]{0:T(128)} %counts_in.1, bf16[512,4608]{1,0:T(8,128)(2,1)} %hid_in.1, bf16[4608,512]{1,0:T(8,128)(2,1)} %wq_in.1, bf16[1024,256]{1,0:T(8,128)(2,1)} %k_in.1, bf16[1024,256]{1,0:T(8,128)(2,1)} %v_in.1, ...), custom_call_target="tpu_custom_call" | custom-call | tf_op jit(solution)/shard_map/layer/pallas_call | solution.py:423
  68.4 1.9 %copy.11 = bf16[64,4608]{1,0:T(8,128)(2,1)} copy(bf16[64,4608]{1,0:T(8,128)(2,1)} %layer.1) | data formatting | bytes 1179648

commit v3 on v2

--- a/solution.py
+++ b/solution.py
@@ -13,8 +13,9 @@
 CTX = 1024
 QR = 512
 HALO = 4
-CH = 64
-NCH = CTX // CH
+CHUNKS = tuple((64 * i, 64) for i in range(15)) + ((960, 32), (992, 32))
+NCH = len(CHUNKS)
+GROUPS = ((0, 4), (4, 8), (8, 12), (12, 14), (14, NCH))
 GR = 256
 NP = 6
 PC = D // NP
@@ -29,7 +30,7 @@
 
 def layer(
     gain_in, post_in, starts_in, counts_in, hid_in, wq_in, k_in, v_in, wo_in, out,
-    gain, post, starts, counts, hid, nrm, wq, kbuf, vbuf, qbuf, acc, att, attr, wo, wp, part, rs_s, rs_r, obuf,
+    gain, post, starts, counts, hid, nrm, wq, kbuf, vbuf, qbuf, acc, att, attr, wo, wp, part, rs_s, rs_r,
     hid_sem, load_sem, kv_s, kv_r, w_s, w_r, att_s, att_r, rss_sem, rsr_sem,
 ):
     s = lax.axis_index("seq")
@@ -96,18 +97,20 @@
     kv_to = {TO_Z: z_up, TO_X: x_near, TO_C1: core, TO_C3: core}
 
     GROUPED = (TO_C1, TO_C3)
-    FIRST_SEM = {TO_Z: 0, TO_X: NCH, TO_C1: 2 * NCH, TO_C3: 2 * NCH + NCH // 4}
+    FIRST_SEM = {TO_Z: 0, TO_X: NCH, TO_C1: 2 * NCH, TO_C3: 2 * NCH + len(GROUPS)}
 
     def kv_send(stream, j, src):
         slot = SLOT[stream]
-        rows = pl.ds(j * CH, CH)
-        arrived = kv_r.at[FIRST_SEM[stream] + (j // 4 if stream in GROUPED else j)]
+        rows = pl.ds(*CHUNKS[j])
+        place = next(g for g, (_, stop) in enumerate(GROUPS) if j < stop) if stream in GROUPED else j
+        arrived = kv_r.at[FIRST_SEM[stream] + place]
         for whole, buf in ((k_in, kbuf), (v_in, vbuf)):
             source = whole.at[rows, :] if src is None else buf.at[src, rows, :]
             remote(source, buf.at[slot, rows, :], kv_s.at[stream], arrived, kv_to[stream]).start()
 
     def kv_wait(stream, j):
-        ref = kbuf.at[SLOT[stream], pl.ds(0, 8 * CH if stream in GROUPED else 2 * CH), :]
+        first, stop = GROUPS[j] if stream in GROUPED else (j, j + 1)
+        ref = kbuf.at[SLOT[stream], pl.ds(0, 2 * sum(n for _, n in CHUNKS[first:stop])), :]
         remote(ref, ref, kv_s.at[stream], kv_r.at[FIRST_SEM[stream] + j], kv_to[stream]).wait_recv()
 
     def kv_sent(stream):
@@ -137,8 +140,31 @@
         W_CB: (1 - parity) * 2 + (1 - c),
     }
 
+    stand_in = [
+        pltpu.make_async_copy(k_in, kbuf.at[4], load_sem.at[8]),
+        pltpu.make_async_copy(v_in, vbuf.at[4], load_sem.at[9]),
+    ]
+    stand_in_x = [
+        pltpu.make_async_copy(k_in, kbuf.at[2], load_sem.at[10]),
+        pltpu.make_async_copy(v_in, vbuf.at[2], load_sem.at[11]),
+    ]
+    first = z == 0
+    first_two = (z * 2 + xl) == 0
+
+    @pl.when(first)
+    def _():
+        for load in stand_in:
+            load.start()
+
+    @pl.when(first_two)
+    def _():
+        for load in stand_in_x:
+            load.start()
+
     for j in range(NCH):
-        kv_send(TO_Z, j, None)
+        @pl.when(z < 3)
+        def _():
+            kv_send(TO_Z, j, None)
 
         @pl.when(xl == 0)
         def _():
@@ -155,9 +181,17 @@
     load_wo.start()
 
     def step_f(j):
-        kv_wait(TO_Z, j)
-
-        @pl.when(xl == 1)
+        @pl.when(z > 0)
+        def _():
+            kv_wait(TO_Z, j)
+
+        if j == 0:
+            @pl.when(first)
+            def _():
+                for load in stand_in:
+                    load.wait()
+
+        @pl.when((xl == 1) & (z > 0))
         def _():
             kv_send(TO_X, j, 4)
 
@@ -166,7 +200,15 @@
             kv_send(TO_C3, j, 4)
 
     def step_g(j):
-        kv_wait(TO_X, j)
+        @pl.when(z * 2 + xl > 0)
+        def _():
+            kv_wait(TO_X, j)
+
+        if j == 0:
+            @pl.when(first_two)
+            def _():
+                for load in stand_in_x:
+                    load.wait()
 
         @pl.when(c == 0)
         def _():
@@ -177,9 +219,8 @@
             kv_send(TO_C1, j, 2)
 
     def step_e(j):
-        if j % 4 == 3:
-            kv_wait(TO_C1, j // 4)
-            kv_wait(TO_C3, j // 4)
+        kv_wait(TO_C1, j)
+        kv_wait(TO_C3, j)
 
     def step_w(j):
         w_copy(W_CROSS, j, mine).wait_recv()
@@ -232,31 +273,37 @@
         source = s - d
         filled[d] = jnp.where(source >= 0, counts[jnp.maximum(source, 0)], 0)
 
-    def attend(base, kh, tile, sources=(1, 2, 3, 0)):
+    def attend(kh, tile, terms):
         lanes = slice(kh * HD, kh * HD + HD)
         rows = slice(tile * 512, tile * 512 + 512)
         q = qbuf[kh, rows, :]
-        row_ids = lax.broadcasted_iota(jnp.int32, (GR, HD), 0)
-
-        def scores(d):
-            key = kbuf[d, base : base + GR, lanes]
+
+        def scores(term):
+            key = [kbuf[d, base : base + n, lanes] for d, base, n in term]
+            key = key[0] if len(key) == 1 else jnp.concatenate(key, axis=0)
             return lax.dot_general(q, key, (((1,), (1,)), ((), ())), preferred_element_type=F32)
 
         def weights(x):
             return jnp.exp2(jnp.tanh(x * (1.0 / 50.0)) * EXP_SCALE)
 
-        def values(d):
-            v = vbuf[d, base : base + GR, lanes]
-            if d == 0:
-                return jnp.concatenate([v, jnp.ones_like(v)], axis=1)
-            keep_row = jnp.where(row_ids < filled[d] - base, 1.0, 0.0).astype(BF)
-            return jnp.concatenate([v * keep_row, keep_row], axis=1)
-
-        pattern = lax.broadcasted_iota(jnp.int32, (128, GR), 1) - lax.broadcasted_iota(jnp.int32, (128, GR), 0)
+        def values(term):
+            out_rows = []
+            for d, base, n in term:
+                v = vbuf[d, base : base + n, lanes]
+                if d == 0:
+                    out_rows.append(jnp.concatenate([v, jnp.ones_like(v)], axis=1))
+                else:
+                    row_ids = lax.broadcasted_iota(jnp.int32, (n, HD), 0)
+                    keep_row = jnp.where(row_ids < filled[d] - base, 1.0, 0.0).astype(BF)
+                    out_rows.append(jnp.concatenate([v * keep_row, keep_row], axis=1))
+            return out_rows[0] if len(out_rows) == 1 else jnp.concatenate(out_rows, axis=0)
+
         total = None
-        for d in sources:
-            if d == 0:
-                near, far = scores(0), scores(4)
+        for term in terms:
+            if term[0][0] == 0:
+                _, base, n = term[0]
+                pattern = lax.broadcasted_iota(jnp.int32, (128, n), 1) - lax.broadcasted_iota(jnp.int32, (128, n), 0)
+                near, far = scores(((0, base, n),)), scores(((4, base, n),))
                 w_near, w_far = [], []
                 for u in range(4):
                     limit = off + block_row((3, 1, 2, 0)[2 * tile + u // 2]) - base
@@ -265,63 +312,74 @@
                     w = weights(jnp.where(is_near, near[part_rows], far[part_rows]))
                     w_near.append(jnp.where(is_near, w, 0.0).astype(BF))
                     w_far.append(jnp.where(is_near, 0.0, w).astype(BF))
-                term = jnp.dot(jnp.concatenate(w_near, axis=0), values(0), preferred_element_type=F32)
-                term = term + jnp.dot(jnp.concatenate(w_far, axis=0), values(4), preferred_element_type=F32)
+                add = jnp.dot(
+                    jnp.concatenate(w_near, axis=0), values(((0, base, n),)), preferred_element_type=F32
+                )
+                add = add + jnp.dot(
+                    jnp.concatenate(w_far, axis=0), values(((4, base, n),)), preferred_element_type=F32
+                )
             else:
-                term = jnp.dot(weights(scores(d)).astype(BF), values(d), preferred_element_type=F32)
-            total = term if total is None else total + term
+                add = jnp.dot(weights(scores(term)).astype(BF), values(term), preferred_element_type=F32)
+            total = add if total is None else total + add
         acc[kh, rows, :] += total
 
-    def units(base, tile, sources=(1, 2, 3, 0)):
+    def single(base, *distances):
+        return tuple(((d, base, GR),) for d in distances)
+
+    def units(tile, terms):
         for kh in range(2):
-            attend(base, kh, tile, sources)
-
-    upto(step_f, 2)
+            attend(kh, tile, terms)
+
+    LAST_A = (((1, 768, 128), (3, 768, 128)),)
+    LAST_B = (((1, 896, 128), (3, 896, 128)),)
+
+    upto(step_f, 4)
     upto(step_w, 1)
-    upto(step_f, 4)
     upto(step_g, 1)
     upto(step_f, 5)
     upto(step_g, 2)
     upto(step_f, 6)
+    upto(step_g, 3)
     upto(step_w, 2)
+    upto(step_f, 7)
     upto(step_g, 4)
-    upto(step_f, 7)
-    upto(step_e, 4)
-    units(0, 0)
+    upto(step_e, 1)
+    units(0, single(0, 1, 2, 3, 0))
     upto(step_f, 9)
     upto(step_g, 5)
     upto(step_z, 1)
-    units(0, 1)
-    upto(step_w, 3)
+    units(1, single(0, 1, 2, 3, 0))
     upto(step_f, 10)
     upto(step_g, 7)
+    upto(step_w, 3)
     upto(step_f, 11)
     upto(step_g, 8)
     upto(step_z, 2)
-    upto(step_e, 8)
-    units(256, 0)
+    upto(step_e, 2)
+    units(0, single(256, 1, 2, 3, 0))
     upto(step_f, 13)
+    upto(step_g, 10)
     upto(step_w, 4)
-    upto(step_g, 10)
-    units(256, 1)
+    units(1, single(256, 1, 2, 3, 0))
     upto(step_f, 14)
     upto(step_g, 11)
-    upto(step_z, 3)
     upto(step_f, 15)
     upto(step_g, 12)
     upto(step_w, 5)
-    upto(step_e, 12)
-    units(512, 0)
-    upto(step_f, 16)
+    upto(step_z, 3)
+    upto(step_e, 3)
+    units(0, single(512, 1, 2, 3, 0))
+    upto(step_f, NCH)
     upto(step_g, 14)
-    units(512, 1)
+    units(0, single(768, 0))
+    upto(step_g, 15)
     upto(step_w, 6)
+    upto(step_e, 4)
+    units(0, LAST_A)
+    upto(step_g, NCH)
     upto(step_z, 4)
-    upto(step_g, 15)
-    units(768, 0, (0,))
-    upto(step_g, 16)
-    units(768, 1, (0, 2))
-    upto(step_e, 16)
+    units(0, single(768, 2))
+    upto(step_e, 5)
 
     def att_copy(slot, kh):
         rows = pl.ds(pl.multiple_of((1 - xh) * 64, 64), 64)
@@ -339,12 +397,13 @@
         for slot in (2 * tile, 2 * tile + 1):
             att_copy(slot, kh).start()
 
-    attend(768, 0, 0, (1, 2, 3))
+    attend(0, 0, LAST_B)
     finish(0, 0)
-    attend(768, 1, 0, (1, 2, 3))
+    attend(1, 0, LAST_B)
     finish(1, 0)
+    units(1, single(512, 1, 2, 3, 0))
     upto(step_z, 5)
-    units(768, 1, (1, 3))
+    units(1, single(768, 1, 2, 3, 0))
     finish(0, 1)
     finish(1, 1)
 
@@ -354,36 +413,44 @@
 
     own_rows = pl.ds(pl.multiple_of(xh * 64, 64), 64)
     load_wo.wait()
-    lhs = jnp.concatenate([att[slot, own_rows, :] for slot in range(4)], axis=0)
-    for p in PIECES:
-        cols = slice(p * PC, p * PC + PC)
-        r = jnp.dot(lhs, wo[:, cols], preferred_element_type=F32)
-        for slot in range(4):
-            part[slot, :, cols] = r[slot * 64 : slot * 64 + 64]
-    for tile in range(2):
+
+    def own_part(tile, p):
+        lhs = jnp.concatenate([att[2 * tile, own_rows, :], att[2 * tile + 1, own_rows, :]], axis=0)
+        return jnp.dot(lhs, wo[:, p * PC : p * PC + PC], preferred_element_type=F32)
+
+    def far_part(tile, p):
+        lhs = jnp.concatenate([attr[2 * tile], attr[2 * tile + 1]], axis=0)
+        return jnp.dot(lhs, wp[:, p * PC : p * PC + PC], preferred_element_type=F32)
+
+    def att_arrived(tile):
         for slot in (2 * tile, 2 * tile + 1):
             for kh in range(2):
                 att_copy(slot, kh).wait_recv()
-        lhs_far = jnp.concatenate([attr[2 * tile], attr[2 * tile + 1]], axis=0)
-        for j, p in enumerate(PIECES):
-            if tile == 0:
-                upto(step_z, j + 1)
-                w_copy(W_CA, j, w_arrives[W_CA]).wait_recv()
-                w_copy(W_CB, j, w_arrives[W_CB]).wait_recv()
-            cols = slice(p * PC, p * PC + PC)
-            r = jnp.dot(lhs_far, wp[:, cols], preferred_element_type=F32)
-            if tile == 0:
-                first, later = (0, 1) if p < NP // 2 else (1, 0)
-                rs_s[0, p] = (part[first, :, cols] + r[first * 64 : first * 64 + 64]).astype(BF)
-                rs_copy(0, p).start()
-                part[later, :, cols] += r[later * 64 : later * 64 + 64]
-            else:
-                part[2, :, cols] += r[:64]
-                part[3, :, cols] += r[64:]
-
+
+    for p in PIECES:
+        cols = slice(p * PC, p * PC + PC)
+        r = own_part(0, p)
+        part[0, :, cols] = r[:64]
+        part[1, :, cols] = r[64:]
+    upto(step_z, 6)
+    att_arrived(0)
+    for j, p in enumerate(PIECES):
+        w_copy(W_CA, j, w_arrives[W_CA]).wait_recv()
+        w_copy(W_CB, j, w_arrives[W_CB]).wait_recv()
+        cols = slice(p * PC, p * PC + PC)
+        r = far_part(0, p)
+        first, later = (0, 1) if p < NP // 2 else (1, 0)
+        rs_s[0, p] = (part[first, :, cols] + r[first * 64 : first * 64 + 64]).astype(BF)
+        rs_copy(0, p).start()
+        part[later, :, cols] += r[later * 64 : later * 64 + 64]
+    att_arrived(1)
     for step in (1, 2):
         for p in PIECES:
             cols = slice(p * PC, p * PC + PC)
+            if step == 1:
+                r = own_part(1, p) + far_part(1, p)
+                part[2, :, cols] = r[:64]
+                part[3, :, cols] = r[64:]
             mine_slot = 2 if step == 1 else (1 if p < NP // 2 else 0)
             rs_copy(step - 1, p).wait_recv()
             rs_s[step, p] = (rs_r[step - 1, p].astype(F32) + part[mine_slot, :, cols]).astype(BF)
@@ -397,15 +464,19 @@
         squares = squares + jnp.sum(whole * whole, axis=-1, keepdims=True)
     factor = lax.rsqrt(squares * (1.0 / D) + 0.1)
     residual_rows = pl.ds(pl.multiple_of(384 + xh * 64, 64), 64)
-    stores = []
     for p in range(NP):
         cols = slice(p * PC, p * PC + PC)
         residual = hid[residual_rows, cols].astype(F32)
-        obuf[:, cols] = (residual + part[3, :, cols] * factor * post[cols].reshape(1, PC)).astype(BF)
-    stores.append(pltpu.make_async_copy(obuf, out, load_sem.at[0]))
-    for store in stores:
-        store.start()
-    for stream in (TO_Z, TO_X, TO_C1, TO_C3):
+        out[:, cols] = (residual + part[3, :, cols] * factor * post[cols].reshape(1, PC)).astype(BF)
+    @pl.when(z < 3)
+    def _():
+        kv_sent(TO_Z)
+
+    @pl.when((xl == 0) | (z > 0))
+    def _():
+        kv_sent(TO_X)
+
+    for stream in (TO_C1, TO_C3):
         kv_sent(stream)
     for stream in (W_CROSS, W_DOWN, W_CA, W_CB):
         w_sent(stream)
@@ -413,8 +484,6 @@
     half = rs_s.at[:, pl.ds(0, NP // 2)]
     remote(half, half, rss_sem.at[0], rsr_sem.at[0, 0], y_up).wait_send()
     remote(half, half, rss_sem.at[1], rsr_sem.at[0, 0], y_down).wait_send()
-    for store in stores:
-        store.wait()
 
 
 def shards(hidden_in, pre_gain, w_query, key_cache, value_cache, w_out, post_gain, starts, counts):
@@ -424,7 +493,7 @@
         layer,
         out_shape=jax.ShapeDtypeStruct((64, D), BF),
         in_specs=[hbm] * 9,
-        out_specs=hbm,
+        out_specs=pl.BlockSpec(memory_space=pltpu.VMEM),
         scratch_shapes=[
             pltpu.VMEM((D,), F32),
             pltpu.VMEM((D,), F32),
@@ -444,11 +513,10 @@
             pltpu.VMEM((4, 64, D), F32),
             pltpu.VMEM((3, NP, 64, PC), BF),
             pltpu.VMEM((3, NP, 64, PC), BF),
-            pltpu.VMEM((64, D), BF),
             dma((4,)),
-            dma((8,)),
+            dma((12,)),
             dma((4,)),
-            dma((2 * NCH + NCH // 2,)),
+            dma((2 * NCH + 2 * len(GROUPS),)),
             dma((4,)),
             dma((4, NP)),
             dma,
@@ -457,12 +525,17 @@
             dma((3, NP)),
         ],
         compiler_params=pltpu.CompilerParams(
-            collective_id=0, has_side_effects=True, vmem_limit_bytes=60 * 1024 * 1024
+            collective_id=0, has_side_effects=True, vmem_limit_bytes=50 * 1024 * 1024
         ),
         name="layer",
     )(
-        pre_gain, post_gain, starts, counts,
-        hidden_in, w_query, key_cache, value_cache, w_out,
+        *[
+            pltpu.with_memory_space_constraint(x, pltpu.HBM)
+            for x in (
+                pre_gain, post_gain, starts, counts,
+                hidden_in, w_query, key_cache, value_cache, w_out,
+            )
+        ]
     )
 
 

time: 70.5 us -> 67.3 us (0.955)
  the two profiles are of different devices: /device:TPU:0 before, /device:TPU:32 now
where the time goes in v3:
time: 67.3 us; the launch traced here: 67.2 us
  Pallas kernels  66.4 us (99%)
  local copies, waits for them, and re-layouts  0.82 us (1%)
    pallas_call x1, Pallas kernels, shards(): pl.pallas_call(layer, out_shape=jax.ShapeDtypeStruct((64, D), BF), in_spe...  66.4 us

profile of v3, /device:TPU:32, one launch (start us, length us, event | category | flops | bytes accessed | tf_op | source)
XLA Modules:
  0.0 67.2 jit_solution(11076286707413844187)
XLA Ops:
  0.0 66.4 %layer.1 = bf16[64,4608]{1,0:T(8,128)(2,1)S(1)} custom-call(f32[4608]{0:T(1024)} %gain_in.1, f32[4608]{0:T(1024)} %post_in.1, s32[16]{0:T(128)} %starts_in.1, s32[16]{0:T(128)} %counts_in.1, bf16[512,4608]{1,0:T(8,128)(2,1)} %hid_in.1, bf16[4608,512]{1,0:T(8,128)(2,1)} %wq_in.1, bf16[1024,256]{1,0:T(8,128)(2,1)} %k_in.1, bf16[1024,256]{1,0:T(8,128)(2,1)} %v_in.1, ...), custom_call_target="tpu_custom_call" | custom-call | tf_op jit(solution)/shard_map/layer/pallas_call | solution.py:492
  66.4 0.8 %copy.11 = bf16[64,4608]{1,0:T(8,128)(2,1)} copy(bf16[64,4608]{1,0:T(8,128)(2,1)S(1)} %layer.1) | data formatting | bytes 1179648

commit v4 on v3

--- a/solution.py
+++ b/solution.py
@@ -13,9 +13,9 @@
 CTX = 1024
 QR = 512
 HALO = 4
-CHUNKS = tuple((64 * i, 64) for i in range(15)) + ((960, 32), (992, 32))
+CHUNKS = ((0, 32), (32, 32)) + tuple((64 * i, 64) for i in range(1, 15)) + ((960, 32), (992, 32))
 NCH = len(CHUNKS)
-GROUPS = ((0, 4), (4, 8), (8, 12), (12, 14), (14, NCH))
+GROUPS = ((0, 5), (5, 9), (9, 13), (13, 15), (15, NCH))
 GR = 256
 NP = 6
 PC = D // NP
@@ -151,6 +151,22 @@
     first = z == 0
     first_two = (z * 2 + xl) == 0
 
+    for j in range(NCH):
+        @pl.when(z < 3)
+        def _():
+            kv_send(TO_Z, j, None)
+
+        @pl.when(xl == 0)
+        def _():
+            kv_send(TO_X, j, None)
+
+        @pl.when(c == 0)
+        def _():
+            kv_send(TO_C1, j, None)
+
+        if j < NP:
+            w_copy(W_CROSS, j, mine, from_input=True).start()
+
     @pl.when(first)
     def _():
         for load in stand_in:
@@ -161,21 +177,6 @@
         for load in stand_in_x:
             load.start()
 
-    for j in range(NCH):
-        @pl.when(z < 3)
-        def _():
-            kv_send(TO_Z, j, None)
-
-        @pl.when(xl == 0)
-        def _():
-            kv_send(TO_X, j, None)
-
-        @pl.when(c == 0)
-        def _():
-            kv_send(TO_C1, j, None)
-
-        if j < NP:
-            w_copy(W_CROSS, j, mine, from_input=True).start()
     load_k.start()
     load_v.start()
     load_wo.start()
@@ -250,17 +251,19 @@
         loads[slot].wait()
         lax.fori_loop(slot * 8, slot * 8 + 8, norm_rows, 0, unroll=4)
     load_wq.wait()
-    for m in range(2):
-        q = jnp.dot(nrm[m * 256 : m * 256 + 256, :], wq[...], preferred_element_type=F32)
+    for slot in range(4):
+        q = jnp.dot(nrm[slot * 128 : slot * 128 + 128, :], wq[...], preferred_element_type=F32)
         q = (q * SCALE).astype(BF)
-        for u in range(2):
-            slot = 2 * m + u
-            for kh in range(2):
-                for g in range(2):
-                    head = 2 * kh + g
-                    qbuf[kh, slot * 256 + g * 128 : slot * 256 + g * 128 + 128, :] = q[
-                        u * 128 : u * 128 + 128, head * HD : head * HD + HD
-                    ]
+        for kh in range(2):
+            for g in range(2):
+                head = 2 * kh + g
+                qbuf[kh, slot * 256 + g * 128 : slot * 256 + g * 128 + 128, :] = q[
+                    :, head * HD : head * HD + HD
+                ]
+        if slot == 1:
+            upto(step_f, 1)
+        if slot == 2:
+            upto(step_f, 2)
     acc[...] = jnp.zeros_like(acc)
     for load in small:
         load.wait()
@@ -333,51 +336,50 @@
     LAST_A = (((1, 768, 128), (3, 768, 128)),)
     LAST_B = (((1, 896, 128), (3, 896, 128)),)
 
-    upto(step_f, 4)
+    upto(step_f, 5)
     upto(step_w, 1)
-    upto(step_g, 1)
-    upto(step_f, 5)
     upto(step_g, 2)
     upto(step_f, 6)
     upto(step_g, 3)
-    upto(step_w, 2)
     upto(step_f, 7)
     upto(step_g, 4)
+    upto(step_f, 8)
+    upto(step_g, 5)
+    upto(step_w, 2)
     upto(step_e, 1)
     units(0, single(0, 1, 2, 3, 0))
-    upto(step_f, 9)
-    upto(step_g, 5)
-    upto(step_z, 1)
+    upto(step_f, 10)
+    upto(step_g, 6)
     units(1, single(0, 1, 2, 3, 0))
-    upto(step_f, 10)
-    upto(step_g, 7)
-    upto(step_w, 3)
     upto(step_f, 11)
     upto(step_g, 8)
-    upto(step_z, 2)
+    upto(step_w, 3)
+    upto(step_f, 12)
+    upto(step_g, 9)
+    upto(step_z, 1)
     upto(step_e, 2)
     units(0, single(256, 1, 2, 3, 0))
-    upto(step_f, 13)
-    upto(step_g, 10)
+    upto(step_f, 14)
+    upto(step_g, 11)
     upto(step_w, 4)
     units(1, single(256, 1, 2, 3, 0))
-    upto(step_f, 14)
-    upto(step_g, 11)
     upto(step_f, 15)
     upto(step_g, 12)
+    upto(step_z, 2)
+    upto(step_f, 16)
+    upto(step_g, 13)
     upto(step_w, 5)
-    upto(step_z, 3)
     upto(step_e, 3)
     units(0, single(512, 1, 2, 3, 0))
     upto(step_f, NCH)
-    upto(step_g, 14)
+    upto(step_g, 15)
+    upto(step_z, 3)
     units(0, single(768, 0))
-    upto(step_g, 15)
-    upto(step_w, 6)
+    upto(step_g, 16)
     upto(step_e, 4)
     units(0, LAST_A)
     upto(step_g, NCH)
-    upto(step_z, 4)
+    upto(step_w, 6)
     units(0, single(768, 2))
     upto(step_e, 5)
 
@@ -401,9 +403,10 @@
     finish(0, 0)
     attend(1, 0, LAST_B)
     finish(1, 0)
+    upto(step_z, 4)
     units(1, single(512, 1, 2, 3, 0))
+    units(1, single(768, 1, 2, 3, 0))
     upto(step_z, 5)
-    units(1, single(768, 1, 2, 3, 0))
     finish(0, 1)
     finish(1, 1)
 
@@ -432,9 +435,10 @@
         r = own_part(0, p)
         part[0, :, cols] = r[:64]
         part[1, :, cols] = r[64:]
-    upto(step_z, 6)
     att_arrived(0)
     for j, p in enumerate(PIECES):
+        if j == 4:
+            upto(step_z, 6)
         w_copy(W_CA, j, w_arrives[W_CA]).wait_recv()
         w_copy(W_CB, j, w_arrives[W_CB]).wait_recv()
         cols = slice(p * PC, p * PC + PC)

time: 67.3 us -> 67.3 us (level)
  no operation moved by 1% of the time
where the time goes in v4:
time: 67.3 us; the launch traced here: 67.2 us
  Pallas kernels  66.3 us (99%)
  local copies, waits for them, and re-layouts  0.82 us (1%)
    pallas_call x1, Pallas kernels, shards(): pl.pallas_call(layer, out_shape=jax.ShapeDtypeStruct((64, D), BF), in_spe...  66.3 us

profile of v4, /device:TPU:32, one launch (start us, length us, event | category | flops | bytes accessed | tf_op | source)
XLA Modules:
  0.0 67.2 jit_solution(7086433109321886361)
XLA Ops:
  0.0 66.3 %layer.1 = bf16[64,4608]{1,0:T(8,128)(2,1)S(1)} custom-call(f32[4608]{0:T(1024)} %gain_in.1, f32[4608]{0:T(1024)} %post_in.1, s32[16]{0:T(128)} %starts_in.1, s32[16]{0:T(128)} %counts_in.1, bf16[512,4608]{1,0:T(8,128)(2,1)} %hid_in.1, bf16[4608,512]{1,0:T(8,128)(2,1)} %wq_in.1, bf16[1024,256]{1,0:T(8,128)(2,1)} %k_in.1, bf16[1024,256]{1,0:T(8,128)(2,1)} %v_in.1, ...), custom_call_target="tpu_custom_call" | custom-call | tf_op jit(solution)/shard_map/layer/pallas_call | solution.py:496
  66.3 0.8 %copy.11 = bf16[64,4608]{1,0:T(8,128)(2,1)} copy(bf16[64,4608]{1,0:T(8,128)(2,1)S(1)} %layer.1) | data formatting | bytes 1179648

commit v5 on v4

--- a/solution.py
+++ b/solution.py
@@ -15,6 +15,8 @@
 HALO = 4
 CHUNKS = ((0, 32), (32, 32)) + tuple((64 * i, 64) for i in range(1, 15)) + ((960, 32), (992, 32))
 NCH = len(CHUNKS)
+DIRECT = (16, 17)
+DIRECT_ROWS = sum(CHUNKS[j][1] for j in DIRECT)
 GROUPS = ((0, 5), (5, 9), (9, 13), (13, 15), (15, NCH))
 GR = 256
 NP = 6
@@ -55,6 +57,7 @@
     core = dev(c_=1 - c)
     x_far = dev(xh_=1 - xh)
     cross = dev(xl_=1 - xl, xh_=1 - xh)
+    diagonal = dev(z_=(z + 3 - 2 * xl) % 4, xl_=1 - xl)
     y_up = dev(y_=(y + 1) % 4)
     y_down = dev(y_=(y + 3) % 4)
 
@@ -85,9 +88,9 @@
         load.start()
 
     barrier = pltpu.get_barrier_semaphore()
-    for other in (z_up, z_down, x_near, core, x_far, cross, y_up, y_down):
+    for other in (z_up, z_down, x_near, core, x_far, cross, diagonal, y_up, y_down):
         pl.semaphore_signal(barrier, inc=1, device_id=other, device_id_type=MESH)
-    pl.semaphore_wait(barrier, 8)
+    pl.semaphore_wait(barrier, 9)
 
     def remote(src, dst, send, recv, to):
         return pltpu.make_async_remote_copy(
@@ -113,9 +116,16 @@
         ref = kbuf.at[SLOT[stream], pl.ds(0, 2 * sum(n for _, n in CHUNKS[first:stop])), :]
         remote(ref, ref, kv_s.at[stream], kv_r.at[FIRST_SEM[stream] + j], kv_to[stream]).wait_recv()
 
-    def kv_sent(stream):
-        ref = kbuf.at[pl.ds(0, 2)]
-        remote(ref, ref, kv_s.at[stream], kv_r.at[FIRST_SEM[stream]], kv_to[stream]).wait_send()
+    def direct_send(j):
+        rows = pl.ds(*CHUNKS[j])
+        arrived = kv_r.at[FIRST_SEM[TO_X] + j]
+        for whole, buf in ((k_in, kbuf), (v_in, vbuf)):
+            remote(whole.at[rows, :], buf.at[SLOT[TO_X], rows, :], kv_s.at[4], arrived, diagonal).start()
+
+    def kv_sent(stream, rows=CTX):
+        ref = kbuf.at[pl.ds(0, 2), pl.ds(0, rows), :]
+        to, first_sem = (diagonal, 0) if stream == 4 else (kv_to[stream], FIRST_SEM[stream])
+        remote(ref, ref, kv_s.at[stream], kv_r.at[first_sem], to).wait_send()
 
     parity = z % 2
     W_CROSS, W_DOWN, W_CA, W_CB = range(4)
@@ -151,6 +161,11 @@
     first = z == 0
     first_two = (z * 2 + xl) == 0
 
+    @pl.when((xl == 1) & (z < 3))
+    def _():
+        for j in DIRECT:
+            direct_send(j)
+
     for j in range(NCH):
         @pl.when(z < 3)
         def _():
@@ -167,19 +182,8 @@
         if j < NP:
             w_copy(W_CROSS, j, mine, from_input=True).start()
 
-    @pl.when(first)
-    def _():
-        for load in stand_in:
-            load.start()
-
-    @pl.when(first_two)
-    def _():
-        for load in stand_in_x:
-            load.start()
-
     load_k.start()
     load_v.start()
-    load_wo.start()
 
     def step_f(j):
         @pl.when(z > 0)
@@ -192,9 +196,10 @@
                 for load in stand_in:
                     load.wait()
 
-        @pl.when((xl == 1) & (z > 0))
-        def _():
-            kv_send(TO_X, j, 4)
+        if j not in DIRECT:
+            @pl.when((xl == 1) & (z > 0))
+            def _():
+                kv_send(TO_X, j, 4)
 
         @pl.when(c == 1)
         def _():
@@ -250,6 +255,17 @@
     for slot in range(4):
         loads[slot].wait()
         lax.fori_loop(slot * 8, slot * 8 + 8, norm_rows, 0, unroll=4)
+    @pl.when(first)
+    def _():
+        for load in stand_in:
+            load.start()
+
+    @pl.when(first_two)
+    def _():
+        for load in stand_in_x:
+            load.start()
+
+    load_wo.start()
     load_wq.wait()
     for slot in range(4):
         q = jnp.dot(nrm[slot * 128 : slot * 128 + 128, :], wq[...], preferred_element_type=F32)
@@ -476,9 +492,17 @@
     def _():
         kv_sent(TO_Z)
 
-    @pl.when((xl == 0) | (z > 0))
+    @pl.when(xl == 0)
     def _():
         kv_sent(TO_X)
+
+    @pl.when((xl == 1) & (z > 0))
+    def _():
+        kv_sent(TO_X, CTX - DIRECT_ROWS)
+
+    @pl.when((xl == 1) & (z < 3))
+    def _():
+        kv_sent(4, DIRECT_ROWS)
 
     for stream in (TO_C1, TO_C3):
         kv_sent(stream)
@@ -519,7 +543,7 @@
             pltpu.VMEM((3, NP, 64, PC), BF),
             dma((4,)),
             dma((12,)),
-            dma((4,)),
+            dma((5,)),
             dma((2 * NCH + 2 * len(GROUPS),)),
             dma((4,)),
             dma((4, NP)),

time: 67.3 us -> 66.7 us (level)
  no operation moved by 1% of the time
where the time goes in v5:
time: 66.7 us; the launch traced here: 66.6 us
  Pallas kernels  65.7 us (99%)
  local copies, waits for them, and re-layouts  0.82 us (1%)
    pallas_call x1, Pallas kernels, shards(): pl.pallas_call(layer, out_shape=jax.ShapeDtypeStruct((64, D), BF), in_spe...  65.7 us

profile of v5, /device:TPU:32, one launch (start us, length us, event | category | flops | bytes accessed | tf_op | source)
XLA Modules:
  0.0 66.6 jit_solution(7605510609985773411)
XLA Ops:
  0.0 65.7 %layer.1 = bf16[64,4608]{1,0:T(8,128)(2,1)S(1)} custom-call(f32[4608]{0:T(1024)} %gain_in.1, f32[4608]{0:T(1024)} %post_in.1, s32[16]{0:T(128)} %starts_in.1, s32[16]{0:T(128)} %counts_in.1, bf16[512,4608]{1,0:T(8,128)(2,1)} %hid_in.1, bf16[4608,512]{1,0:T(8,128)(2,1)} %wq_in.1, bf16[1024,256]{1,0:T(8,128)(2,1)} %k_in.1, bf16[1024,256]{1,0:T(8,128)(2,1)} %v_in.1, ...), custom_call_target="tpu_custom_call" | custom-call | tf_op jit(solution)/shard_map/layer/pallas_call | solution.py:520
  65.8 0.8 %copy.11 = bf16[64,4608]{1,0:T(8,128)(2,1)} copy(bf16[64,4608]{1,0:T(8,128)(2,1)S(1)} %layer.1) | data formatting | bytes 1179648

commit v6 on v5

--- a/solution.py
+++ b/solution.py
@@ -161,26 +161,27 @@
     first = z == 0
     first_two = (z * 2 + xl) == 0
 
+    for j in range(NCH):
+        @pl.when(z < 3)
+        def _():
+            kv_send(TO_Z, j, None)
+
+        @pl.when(xl == 0)
+        def _():
+            kv_send(TO_X, j, None)
+
+        @pl.when(c == 0)
+        def _():
+            kv_send(TO_C1, j, None)
+
+        if j < NP:
+            w_copy(W_CROSS, j, mine, from_input=True).start()
+
+
     @pl.when((xl == 1) & (z < 3))
     def _():
         for j in DIRECT:
             direct_send(j)
-
-    for j in range(NCH):
-        @pl.when(z < 3)
-        def _():
-            kv_send(TO_Z, j, None)
-
-        @pl.when(xl == 0)
-        def _():
-            kv_send(TO_X, j, None)
-
-        @pl.when(c == 0)
-        def _():
-            kv_send(TO_C1, j, None)
-
-        if j < NP:
-            w_copy(W_CROSS, j, mine, from_input=True).start()
 
     load_k.start()
     load_v.start()

time: 66.7 us -> 66.8 us (level)
  no operation moved by 1% of the time
where the time goes in v6:
time: 66.8 us; the launch traced here: 66.7 us
  Pallas kernels  65.9 us (99%)
  local copies, waits for them, and re-layouts  0.82 us (1%)
    pallas_call x1, Pallas kernels, shards(): pl.pallas_call(layer, out_shape=jax.ShapeDtypeStruct((64, D), BF), in_spe...  65.9 us

profile of v6, /device:TPU:32, one launch (start us, length us, event | category | flops | bytes accessed | tf_op | source)
XLA Modules:
  0.0 66.7 jit_solution(9051658294695540238)
XLA Ops:
  0.0 65.9 %layer.1 = bf16[64,4608]{1,0:T(8,128)(2,1)S(1)} custom-call(f32[4608]{0:T(1024)} %gain_in.1, f32[4608]{0:T(1024)} %post_in.1, s32[16]{0:T(128)} %starts_in.1, s32[16]{0:T(128)} %counts_in.1, bf16[512,4608]{1,0:T(8,128)(2,1)} %hid_in.1, bf16[4608,512]{1,0:T(8,128)(2,1)} %wq_in.1, bf16[1024,256]{1,0:T(8,128)(2,1)} %k_in.1, bf16[1024,256]{1,0:T(8,128)(2,1)} %v_in.1, ...), custom_call_target="tpu_custom_call" | custom-call | tf_op jit(solution)/shard_map/layer/pallas_call | solution.py:521
  65.9 0.8 %copy.11 = bf16[64,4608]{1,0:T(8,128)(2,1)} copy(bf16[64,4608]{1,0:T(8,128)(2,1)S(1)} %layer.1) | data formatting | bytes 1179648
